TPU v7x, 32 devices: a whole 2x2x4 slice. The times are simulated.
32 devices in a mesh: dp: 8 (over y, x, core), mp: 4 (over z).
Axes of the slice: x: 2, y: 2, z: 4, core: 2. Of those that a mesh axis runs over, the one named last changes fastest.
Arguments:
- inputs: bfloat16 [8192, 2048], P(('dp', 'mp')), may hold values from -6 to 6
- segments: int32 [8, 1024], P('dp'), may hold values from 0 to 5, never falling along the last dimension, each value on 1 to 512 neighbouring positions
- first_norm_gain: float32 [2048], replicated, may hold values from 0.1 to 1.9
- w_query: bfloat16 [2048, 2048], P('dp', 'mp'), may hold values from -0.125 to 0.125
- w_key: bfloat16 [2048, 2048], P('dp', 'mp'), may hold values from -0.125 to 0.125
- w_value: bfloat16 [2048, 3456], P('dp', 'mp'), may hold values from -0.125 to 0.125
- w_gate: bfloat16 [2048, 3456], P('dp', 'mp'), may hold values from -0.125 to 0.125
- w_out: bfloat16 [3456, 2048], P('mp', 'dp'), may hold values from -0.21875 to 0.21875
- second_norm_gain: float32 [2048], replicated, may hold values from 0.1 to 1.9
- w_glu_gate: bfloat16 [2048, 3456], P('dp', 'mp'), may hold values from -0.125 to 0.125
- w_glu_up: bfloat16 [2048, 3456], P('dp', 'mp'), may hold values from -0.125 to 0.125
- w_down: bfloat16 [3456, 2048], P('mp', 'dp'), may hold values from -0.21875 to 0.21875
- cotangent: bfloat16 [8192, 2048], P(('dp', 'mp')), may hold values from -9 to 9
Outputs:
- outputs: bfloat16 [8192, 2048], P(('dp', 'mp'))
- input_gradient: float32 [8192, 2048], P(('dp', 'mp'))
- grad_norm1_gain: float32 [2048], replicated
- grad_w_query: float32 [2048, 2048], P('dp', 'mp')
- grad_w_key: float32 [2048, 2048], P('dp', 'mp')
- grad_w_value: float32 [2048, 3456], P('dp', 'mp')
- grad_w_gate: float32 [2048, 3456], P('dp', 'mp')
- grad_w_out: float32 [3456, 2048], P('mp', 'dp')
- grad_norm2_gain: float32 [2048], replicated
- grad_w_glu_gate: float32 [2048, 3456], P('dp', 'mp')
- grad_w_glu_up: float32 [2048, 3456], P('dp', 'mp')
- grad_w_down: float32 [3456, 2048], P('mp', 'dp')
Inputs may be any that keep to these rules, and one draw needn't show every extreme that they name: `segments`: within a sequence the document numbers never fall; each document holds 1 to 512 tokens and one holds exactly 512.
All inputs are finite; a program needn't handle non-finite values.
Results may differ from a plain program's by a relative error of at most 0.024.
Values may be sent and summed in bfloat16 or wider, within the bound.
A program may use at most 256 MiB of HBM per device.

v0:
```python
import jax
import jax.numpy as jnp
from jax import lax
from jax.sharding import PartitionSpec as P

H = 8
HK = 256
HV = 432
LEN = 1024
CHUNKS = 2
epsilon = 1e-05
group_epsilon = 1.0
BF = jnp.bfloat16
F32 = jnp.float32


def layer_norm(values_in, offset):
    centre = jnp.mean(values_in, axis=-1, keepdims=True)
    centred = values_in - centre
    variance = jnp.mean(centred * centred, axis=-1, keepdims=True)
    scaling = lax.rsqrt(variance + offset)
    return (centred * scaling, scaling)


def norm_back(grad_hat, normed_hat, scaling):
    first_mean = jnp.mean(grad_hat, axis=-1, keepdims=True)
    second_mean = jnp.mean(grad_hat * normed_hat, axis=-1, keepdims=True)
    return scaling * (grad_hat - first_mean - normed_hat * second_mean)


def glu_act(gate_pre, up_pre):
    return jax.nn.gelu(gate_pre, approximate=True) * up_pre


def dot_nt(a, b):
    return lax.dot_general(a, b, (((1,), (1,)), ((), ())), preferred_element_type=F32)


def dot_nn(a, b):
    return lax.dot_general(a, b, (((1,), (0,)), ((), ())), preferred_element_type=F32)


def dot_tn(a, b):
    return lax.dot_general(a, b, (((0,), (0,)), ((), ())), preferred_element_type=F32)


def line_gather(own, n, place):
    right, left = ([None], [None])
    r = l = own
    for step in range(1, n):
        r = lax.ppermute(r, "mp", [(i, i + 1) for i in range(step - 1, n - 1)])
        l = lax.ppermute(l, "mp", [(i, i - 1) for i in range(1, n - step + 1)])
        right.append(r)
        left.append(l)
    return [own] + [jnp.where(place >= k, right[k], left[n - k]) for k in range(1, n)]


def line_scatter(slots, n):
    r = l = None
    for step in range(1, n):
        send_r, send_l = (slots[step], slots[n - step])
        if r is not None:
            send_r = (send_r.astype(F32) + r.astype(F32)).astype(BF)
            send_l = (send_l.astype(F32) + l.astype(F32)).astype(BF)
        r = lax.ppermute(send_r, "mp", [(i, i + 1) for i in range(step)])
        l = lax.ppermute(send_l, "mp", [(i, i - 1) for i in range(n - step, n)])
    return slots[0].astype(F32) + r.astype(F32) + l.astype(F32)


def body(
    inputs,
    segments,
    first_norm_gain,
    w_query,
    w_key,
    w_value,
    w_gate,
    w_out,
    second_norm_gain,
    w_glu_gate,
    w_glu_up,
    w_down,
    cotangent,
):
    n = lax.axis_size("mp")
    place = lax.axis_index("mp")
    heads = H // n
    head_start = place * heads
    rows, width = inputs.shape
    piece = rows // CHUNKS
    per = n * piece
    nk, nv, nf = (heads * HK, heads * HV, w_down.shape[0])
    pack_one = jnp.concatenate([w_query.T, w_key.T, w_value.T, w_gate.T], axis=0)
    weight_one = lax.all_gather(pack_one, "dp", axis=1, tiled=True)
    out_weight = lax.all_gather(w_out, "dp", axis=1, tiled=True)
    pack_two = jnp.concatenate([w_glu_gate.T, w_glu_up.T, w_down], axis=0)
    weight_two = lax.all_gather(pack_two, "dp", axis=1, tiled=True)
    glu_weight, down_weight = (weight_two[: 2 * nf], weight_two[2 * nf :])

    def cut(array):
        return [array[h * piece : (h + 1) * piece] for h in range(CHUNKS)]

    def gather(block):
        return jnp.concatenate(line_gather(block, n, place), axis=0)

    def scatter(part):
        return line_scatter([part[k * piece : (k + 1) * piece] for k in range(n)], n)

    inputs_cut = [c.astype(F32) for c in cut(inputs)]
    first_hat, first_scale, first_rows = ([], [], [])
    for x in inputs_cut:
        hat, scale = layer_norm(x, epsilon)
        first_hat.append(hat)
        first_scale.append(scale)
        first_rows.append((hat * first_norm_gain).astype(BF))
    rows_one = jnp.concatenate([gather(block) for block in first_rows], axis=0)
    tokens = rows_one.shape[0]
    slot_shard = lax.rem(place - jnp.arange(n) + n, n)
    places = (
        slot_shard[None, :, None] * rows
        + jnp.arange(CHUNKS)[:, None, None] * piece
        + jnp.arange(piece)[None, None, :]
    ).reshape(tokens)
    seg = segments.reshape(n, CHUNKS, piece)[::-1]
    seg = lax.dynamic_slice_in_dim(jnp.concatenate([seg, seg], axis=0), n - 1 - place, n, axis=0)
    seg = seg.transpose(1, 0, 2).reshape(tokens)
    query_key = dot_nt(rows_one, weight_one[: 2 * nk]).astype(BF)
    value = dot_nt(rows_one, weight_one[2 * nk : 2 * nk + nv]).astype(BF)
    gate_pre = dot_nt(rows_one, weight_one[2 * nk + nv :])
    query = query_key[:, :nk].reshape(tokens, heads, HK)
    key = query_key[:, nk:].reshape(tokens, heads, HK)
    value = value.reshape(tokens, heads, HV)
    distance = places[:, None] - places[None, :]
    allowed = (distance >= 0) & (seg[:, None] == seg[None, :])
    log_gamma = jnp.log1p(-jnp.exp2(-5.0 - (head_start + jnp.arange(heads)).astype(F32)))
    exponent = jnp.where(allowed[None], distance[None].astype(F32) * log_gamma[:, None, None], 0.0)
    mask = jnp.where(allowed[None], jnp.exp(exponent), 0.0) * HK ** (-0.5)
    scores = (jnp.einsum("thk,shk->hts", query, key, preferred_element_type=F32) * mask).astype(BF)
    retained = jnp.einsum("hts,shv->thv", scores, value, preferred_element_type=F32)
    normalized, scale_group = layer_norm(retained, group_epsilon)
    normal_flat = normalized.reshape(tokens, nv)
    swish = jax.nn.silu(gate_pre)
    gated = (swish * normal_flat).astype(BF)
    cot_cut = cut(cotangent)
    cot_rows = [gather(c) for c in cot_cut]

    def group(array, h):
        return array[h * per : (h + 1) * per]

    outputs, second_gain, middle_grad = ([], [], [])
    rows_two, hidden_all, d_glu_all, mid_rows = ([], [], [], [])
    for h in range(CHUNKS):
        attn_part = dot_nn(group(gated, h), out_weight).astype(BF)
        middle = inputs_cut[h] + scatter(attn_part)
        hat, scale = layer_norm(middle, epsilon)
        rows_h = gather((hat * second_norm_gain).astype(BF))
        rows_two.append(rows_h)
        glu = dot_nt(rows_h, glu_weight)
        glu_gate, glu_up = (glu[:, :nf], glu[:, nf:])
        d_hidden = dot_nt(cot_rows[h], down_weight)
        hidden, pullback = jax.vjp(glu_act, glu_gate, glu_up)
        hidden = hidden.astype(BF)
        d_glu = jnp.concatenate([d.astype(BF) for d in pullback(d_hidden)], axis=1)
        hidden_all.append(hidden)
        d_glu_all.append(d_glu)
        second_grad = scatter(dot_nn(d_glu, glu_weight).astype(BF))
        second_gain.append(jnp.sum(hat * second_grad, axis=0))
        grad_h = cot_cut[h].astype(F32) + norm_back(second_grad * second_norm_gain, hat, scale)
        middle_grad.append(grad_h)
        mid_rows.append(gather(grad_h.astype(BF)))
        outputs.append(middle + scatter(dot_nn(hidden, down_weight).astype(BF)))
    cot_all = jnp.concatenate(cot_rows, axis=0)
    grads_two = jnp.concatenate(
        [
            dot_tn(jnp.concatenate(d_glu_all, axis=0), jnp.concatenate(rows_two, axis=0)),
            dot_tn(jnp.concatenate(hidden_all, axis=0), cot_all),
        ],
        axis=0,
    ).astype(BF)
    summed_two = lax.psum_scatter(grads_two, "dp", scatter_dimension=1, tiled=True).astype(F32)
    mid_all = jnp.concatenate(mid_rows, axis=0)
    d_gated = dot_nt(mid_all, out_weight)
    sigmoid_gate = jax.nn.sigmoid(gate_pre)
    d_gate_pre = (
        d_gated * normal_flat * (sigmoid_gate + gate_pre * sigmoid_gate * (1.0 - sigmoid_gate))
    ).astype(BF)
    d_normalized = (d_gated * swish).reshape(tokens, heads, HV)
    d_retained = norm_back(d_normalized, normalized, scale_group).astype(BF)
    grads_out = jnp.concatenate(
        [dot_tn(gated, mid_all).astype(BF), dot_tn(d_gate_pre, rows_one).astype(BF)], axis=0
    )
    summed_out = lax.psum_scatter(grads_out, "dp", scatter_dimension=1, tiled=True).astype(F32)
    d_value = jnp.einsum("hts,thv->shv", scores, d_retained, preferred_element_type=F32).astype(BF)
    d_scores = (
        jnp.einsum("thv,shv->hts", d_retained, value, preferred_element_type=F32) * mask
    ).astype(BF)
    d_query = jnp.einsum("hts,shk->thk", d_scores, key, preferred_element_type=F32).astype(BF)
    d_key = jnp.einsum("hts,thk->shk", d_scores, query, preferred_element_type=F32).astype(BF)
    d_qkv = jnp.concatenate(
        [d_query.reshape(tokens, nk), d_key.reshape(tokens, nk), d_value.reshape(tokens, nv)],
        axis=1,
    )
    grads_one = dot_tn(d_qkv, rows_one).astype(BF)
    summed_one = lax.psum_scatter(grads_one, "dp", scatter_dimension=1, tiled=True).astype(F32)
    d_one = jnp.concatenate([d_qkv, d_gate_pre], axis=1)
    input_gradient, first_gain = ([], [])
    for h in range(CHUNKS):
        first_grad = scatter(dot_nn(group(d_one, h), weight_one).astype(BF))
        first_gain.append(jnp.sum(first_hat[h] * first_grad, axis=0))
        input_gradient.append(
            middle_grad[h] + norm_back(first_grad * first_norm_gain, first_hat[h], first_scale[h])
        )
    gains = lax.psum(jnp.stack([sum(first_gain), sum(second_gain)]), ("dp", "mp"))
    return (
        jnp.concatenate(outputs, axis=0).astype(BF),
        jnp.concatenate(input_gradient, axis=0),
        gains[0],
        summed_one[:nk].T,
        summed_one[nk : 2 * nk].T,
        summed_one[2 * nk :].T,
        summed_out[nv:].T,
        summed_out[:nv],
        gains[1],
        summed_two[:nf].T,
        summed_two[nf : 2 * nf].T,
        summed_two[2 * nf :],
    )


def solution(mesh):
    split = P(("dp", "mp"), None)
    wide, tall = (P("dp", "mp"), P("mp", "dp"))
    return jax.shard_map(
        body,
        mesh=mesh,
        in_specs=(
            split,
            P("dp", None),
            P(),
            wide,
            wide,
            wide,
            wide,
            tall,
            P(),
            wide,
            wide,
            tall,
            split,
        ),
        out_specs=(split, split, P(), wide, wide, wide, wide, tall, P(), wide, wide, tall),
        check_vma=False,
    )
```

profile of v0, /device:TPU:0, one launch (start us, length us, event | category | flops | bytes accessed | tf_op | source)
XLA Modules:
  0.0 846.9 jit_solution(8839183228155669539)
XLA Ops:
  15.7 5.6 collective-permute-start
  21.3 10.0 %collective-permute-done.1 = bf16[128,2048]{1,0:T(8,128)(2,1)S(1)} collective-permute-done((bf16[128,2048]{1,0:T(8,128)(2,1)S(1)}, bf16[128,2048]{1,0:T(8,128)(2,1)S(1)}, u32[]{:S(2)}, u32[]{:S(2)}) %collective-permute-start.1) | collective-permute-done | bytes 524320 | tf_op jit(solution)/shard_map/ppermute | solution.py:52
  33.3 13.1 %collective-permute-done.2 = bf16[128,2048]{1,0:T(8,128)(2,1)S(1)} collective-permute-done((bf16[128,2048]{1,0:T(8,128)(2,1)S(1)}, bf16[128,2048]{1,0:T(8,128)(2,1)S(1)}, u32[]{:S(2)}, u32[]{:S(2)}) %collective-permute-start.2) | collective-permute-done | bytes 524320 | tf_op jit(solution)/shard_map/ppermute | solution.py:52
  48.6 12.1 %collective-permute-done.3 = bf16[128,2048]{1,0:T(8,128)(2,1)} collective-permute-done((bf16[128,2048]{1,0:T(8,128)(2,1)S(1)}, bf16[128,2048]{1,0:T(8,128)(2,1)}, u32[]{:S(2)}, u32[]{:S(2)}) %collective-permute-start.3) | collective-permute-done | bytes 524320 | tf_op jit(solution)/shard_map/ppermute | solution.py:52
  68.4 4.6 collective-permute-start.6
  73.0 6.1 collective-permute-done.7
  83.5 8.2 collective-permute-done.8
  95.1 8.5 %collective-permute-done.9 = bf16[128,2048]{1,0:T(8,128)(2,1)} collective-permute-done((bf16[128,2048]{1,0:T(8,128)(2,1)S(1)}, bf16[128,2048]{1,0:T(8,128)(2,1)}, u32[]{:S(2)}, u32[]{:S(2)}) %collective-permute-start.9) | collective-permute-done | bytes 524320 | tf_op jit(solution)/shard_map/ppermute | solution.py:52
  107.4 8.1 fusion.74
  118.5 4.9 multiply_convert_fusion.1
  132.7 6.0 fusion.27
  138.7 4.8 convolution_convert_fusion.8
  150.5 6.6 collective-permute-done.30
  162.6 5.8 collective-permute-done.12
  185.8 5.1 collective-permute-done.13
  197.0 8.1 collective-permute-start.48
  206.4 6.9 collective-permute-done.14
  221.1 17.0 %collective-permute-start.18 = (bf16[128,2048]{1,0:T(8,128)(2,1)S(1)}, bf16[128,2048]{1,0:T(8,128)(2,1)S(1)}, u32[]{:S(2)}, u32[]{:S(2)}) collective-permute-start(bf16[128,2048]{1,0:T(8,128)(2,1)S(1)} %get-tuple-element.72), channel_id=1, source_target_pairs={{0,1},{1,2},{2,3},{4,5},{5,6},{6,7},{8,9},{9,10},{10,11},{12,13},{... | collective-permute-start | bytes 1572872 | tf_op jit(solution)/shard_map/ppermute | solution.py:51
  240.2 8.6 %collective-permute-done.51 = bf16[128,2048]{1,0:T(8,128)(2,1)S(1)} collective-permute-done((bf16[128,2048]{1,0:T(8,128)(2,1)S(1)}, bf16[128,2048]{1,0:T(8,128)(2,1)S(1)}, u32[]{:S(2)}, u32[]{:S(2)}) %collective-permute-start.51) | collective-permute-done | bytes 524320 | tf_op jit(solution)/shard_map/ppermute | solution.py:52
  250.3 5.2 collective-permute-done.20
  259.9 7.3 collective-permute-done.21
  270.7 7.8 fusion.6
  293.0 7.0 collective-permute-done.54
  309.0 16.9 %collective-permute-start.25 = (bf16[128,2048]{1,0:T(8,128)(2,1)S(1)}, bf16[128,2048]{1,0:T(8,128)(2,1)S(1)}, u32[]{:S(2)}, u32[]{:S(2)}) collective-permute-start(bf16[128,2048]{1,0:T(8,128)(2,1)S(1)} %get-tuple-element.135), channel_id=1, source_target_pairs={{0,1},{1,2},{4,5},{5,6},{8,9},{9,10},{12,13},{13,14},{16,17},{17,1... | collective-permute-start | bytes 1572872 | tf_op jit(solution)/shard_map/ppermute | solution.py:65
  327.3 12.0 %collective-permute-start.56 = (bf16[128,2048]{1,0:T(8,128)(2,1)S(1)}, bf16[128,2048]{1,0:T(8,128)(2,1)S(1)}, u32[]{:S(2)}, u32[]{:S(2)}) collective-permute-start(bf16[128,2048]{1,0:T(8,128)(2,1)S(1)} %get-tuple-element.127), channel_id=1, source_target_pairs={{0,1},{1,2},{2,3},{4,5},{5,6},{6,7},{8,9},{9,10},{10,11},{12,13},{... | collective-permute-start | bytes 1572872 | tf_op jit(solution)/shard_map/ppermute | solution.py:65
  341.1 10.1 %collective-permute-start.26 = (bf16[128,2048]{1,0:T(8,128)(2,1)S(1)}, bf16[128,2048]{1,0:T(8,128)(2,1)S(1)}, u32[]{:S(2)}, u32[]{:S(2)}) collective-permute-start(bf16[128,2048]{1,0:T(8,128)(2,1)S(1)} %get-tuple-element.133), channel_id=1, source_target_pairs={{0,1},{1,2},{2,3},{4,5},{5,6},{6,7},{8,9},{9,10},{10,11},{12,13},{... | collective-permute-start | bytes 1572872 | tf_op jit(solution)/shard_map/ppermute | solution.py:65
  357.8 12.8 %collective-permute-done.29 = bf16[128,2048]{1,0:T(8,128)(2,1)S(1)} collective-permute-done((bf16[128,2048]{1,0:T(8,128)(2,1)S(1)}, bf16[128,2048]{1,0:T(8,128)(2,1)S(1)}, u32[]{:S(2)}, u32[]{:S(2)}) %collective-permute-start.29) | collective-permute-done | bytes 524320 | tf_op jit(solution)/shard_map/ppermute | solution.py:66
  377.5 5.2 collective-permute-start.66
  384.0 4.6 collective-permute-start.36
  392.8 9.9 %collective-permute-done.61 = bf16[128,2048]{1,0:T(8,128)(2,1)S(1)} collective-permute-done((bf16[128,2048]{1,0:T(8,128)(2,1)S(1)}, bf16[128,2048]{1,0:T(8,128)(2,1)S(1)}, u32[]{:S(2)}, u32[]{:S(2)}) %collective-permute-start.61) | collective-permute-done | bytes 524320 | tf_op jit(solution)/shard_map/ppermute | solution.py:52
  405.5 8.5 %collective-permute-done.37 = bf16[128,2048]{1,0:T(8,128)(2,1)S(1)} collective-permute-done((bf16[128,2048]{1,0:T(8,128)(2,1)S(1)}, bf16[128,2048]{1,0:T(8,128)(2,1)S(1)}, u32[]{:S(2)}, u32[]{:S(2)}) %collective-permute-start.37) | collective-permute-done | bytes 524320 | tf_op jit(solution)/shard_map/ppermute | solution.py:52
  416.0 9.2 %collective-permute-done.68 = bf16[128,2048]{1,0:T(8,128)(2,1)S(1)} collective-permute-done((bf16[128,2048]{1,0:T(8,128)(2,1)S(1)}, bf16[128,2048]{1,0:T(8,128)(2,1)S(1)}, u32[]{:S(2)}, u32[]{:S(2)}) %collective-permute-start.68) | collective-permute-done | bytes 524320 | tf_op jit(solution)/shard_map/ppermute | solution.py:52
  428.6 7.7 collective-permute-done.38
  444.4 8.7 %collective-permute-done.39 = bf16[128,2048]{1,0:T(8,128)(2,1)S(1)} collective-permute-done((bf16[128,2048]{1,0:T(8,128)(2,1)S(1)}, bf16[128,2048]{1,0:T(8,128)(2,1)S(1)}, u32[]{:S(2)}, u32[]{:S(2)}) %collective-permute-start.39) | collective-permute-done | bytes 524320 | tf_op jit(solution)/shard_map/ppermute | solution.py:52
  456.8 7.2 fusion.4
  464.0 5.3 fusion.90
  469.4 5.3 convolution_convert_fusion.7
  477.0 7.2 fusion.34
  494.4 5.4 collective-permute-done.72
  500.8 5.0 collective-permute-start.73
  511.4 4.8 collective-permute-start.44
  521.7 5.2 collective-permute-start.74
  529.2 6.3 collective-permute-done.74
  535.5 6.1 collective-permute-done.77
  546.8 7.6 collective-permute-start.78
  554.4 6.6 collective-permute-done.79
  563.0 9.1 %collective-permute-done.80 = bf16[128,2048]{1,0:T(8,128)(2,1)S(1)} collective-permute-done((bf16[128,2048]{1,0:T(8,128)(2,1)S(1)}, bf16[128,2048]{1,0:T(8,128)(2,1)S(1)}, u32[]{:S(2)}, u32[]{:S(2)}) %collective-permute-start.80) | collective-permute-done | bytes 524320 | tf_op jit(solution)/shard_map/ppermute | solution.py:52
  574.1 9.1 %collective-permute-done.81 = bf16[128,2048]{1,0:T(8,128)(2,1)S(1)} collective-permute-done((bf16[128,2048]{1,0:T(8,128)(2,1)S(1)}, bf16[128,2048]{1,0:T(8,128)(2,1)S(1)}, u32[]{:S(2)}, u32[]{:S(2)}) %collective-permute-start.81) | collective-permute-done | bytes 524320 | tf_op jit(solution)/shard_map/ppermute | solution.py:52
  583.6 5.3 convolution_convert_fusion.4
  588.9 6.6 fusion.159
  596.8 5.3 convolution_convert_fusion.3
  602.1 7.3 pad_maximum_fusion.1
  628.1 13.3 %convolution_convert_fusion.1 = bf16[1888,2048]{1,0:T(8,128)(2,1)} fusion(bf16[1024,2048]{1,0:T(8,128)(2,1)S(1)} %copy-done.50, bf16[1024,864]{0,1:T(8,128)(2,1)S(1)} %bitcast.92, bf16[1024,512]{0,1:T(8,128)(2,1)S(1)} %bitcast.100, bf16[1024,512]{0,1:T(8,128)(2,1)S(1)} %bitcast.102), kind=kOutput, calls=%fused_computation.5 | convolution fusion | flops 7934312448 | bytes 15794176 | tf_op jit(solution)/shard_map/dot_general | solution.py:44
  641.8 6.7 convolution_convert_fusion.2
  648.5 21.0 %convolution_convert_fusion = bf16[1728,2048]{1,0:T(8,128)(2,1)S(1)} fusion(bf16[1024,2048]{1,0:T(8,128)(2,1)} %get-tuple-element.57, bf16[512,864]{0,1:T(8,128)(2,1)S(1)} %copy-done.88, bf16[512,864]{0,1:T(8,128)(2,1)S(1)} %copy-done.86, bf16[512,864]{0,1:T(8,128)(2,1)S(1)} %copy-done.84, bf16[512,864]{0,1:T(8,128)(2,1)S(1)} %copy-done.82), kind=kOutput, calls=%fused_computation.4 | convolution fusion | flops 7265452032 | bytes 14811136 | tf_op jit(solution)/shard_map/dot_general | solution.py:44
  669.5 12.8 %pad_maximum_fusion = bf16[2592,2048]{1,0:T(8,128)(2,1)} fusion(bf16[864,2048]{1,0:T(8,128)(2,1)S(1)} %convolution_convert_fusion.2, bf16[1728,2048]{1,0:T(8,128)(2,1)S(1)} %convolution_convert_fusion), kind=kLoop, calls=%fused_computation | loop fusion | flops 21233664 | bytes 21233664 | tf_op jit(solution)/shard_map/concatenate | solution.py:173
  688.1 10.2 %convolution_convert_fusion.6 = bf16[512,2048]{1,0:T(8,128)(2,1)S(1)} fusion(bf16[2752,2048]{1,0:T(8,128)(2,1)} %all-gather.4.cloned.1.call-done, bf16[1024,2752]{0,1:T(8,128)(2,1)S(1)} %pad_maximum_fusion.2), kind=kOutput, calls=%fused_computation.55 | convolution fusion | flops 5772410880 | bytes 16187392 | tf_op jit(solution)/shard_map/dot_general | solution.py:40
  700.5 6.6 convolution_convert_fusion.5
  717.4 5.8 collective-permute-done.90
  723.6 4.5 collective-permute-start.91
  729.0 5.3 collective-permute-done.85
  740.9 7.9 collective-permute-start.92
  761.2 40.4 %psum.7 = f32[2,2048]{1,0:T(2,128)S(1)} all-reduce(f32[2,2048]{1,0:T(2,128)S(1)} %pad_maximum_fusion.7), channel_id=1, replica_groups=mesh['dp'=8,'mp'=4] {'dp','mp'}, use_global_device_ids=true, to_apply=%region_24.25 | all-reduce | flops 4096 | bytes 32768 | tf_op jit(solution)/shard_map/psum | solution.py:213
  815.8 19.9 %reduce-scatter.8.cloned.1.call-done = bf16[2592,256]{1,0:T(8,128)(2,1)} async-done(((bf16[2592,2048]{1,0:T(8,128)(2,1)}), bf16[2592,256]{1,0:T(8,128)(2,1)}) %reduce-scatter.8.cloned.1.call-update) | async-done | bytes 1327120 | tf_op jit(solution)/shard_map/reduce_scatter | solution.py:180
  (487 shorter events, 277.3 us)
Async XLA Ops:
  7.2 100.2 %all-gather.4.cloned.1.call-start = ((), (), s32[]{:S(2)}) async-start(), calls=%async_computation.3 | async-start | bytes 12681216 | tf_op jit(solution)/shard_map/all_gather | solution.py:94
  11.9 126.8 %all-gather.6.cloned.1.call-start = ((), (), s32[]{:S(2)}) async-start(), calls=%async_computation.4 | async-start | bytes 3981312 | tf_op jit(solution)/shard_map/all_gather | solution.py:95
  12.6 258.0 %all-gather.8.cloned.1.call-start = ((), (), s32[]{:S(2)}) async-start(), calls=%async_computation.5 | async-start | bytes 11943936 | tf_op jit(solution)/shard_map/all_gather | solution.py:97
  14.4 16.9 %collective-permute-start.1 = (bf16[128,2048]{1,0:T(8,128)(2,1)S(1)}, bf16[128,2048]{1,0:T(8,128)(2,1)S(1)}, u32[]{:S(2)}, u32[]{:S(2)}) collective-permute-start(bf16[128,2048]{1,0:T(8,128)(2,1)S(1)} %get-tuple-element.98), channel_id=1, source_target_pairs={{1,0},{2,1},{3,2},{5,4},{6,5},{7,6},{9,8},{10,9},{11,10},{13,12},{... | collective-permute-start | bytes 1572872 | tf_op jit(solution)/shard_map/ppermute | solution.py:52
  15.7 16.9 %collective-permute-start = (bf16[128,2048]{1,0:T(8,128)(2,1)S(1)}, bf16[128,2048]{1,0:T(8,128)(2,1)S(1)}, u32[]{:S(2)}, u32[]{:S(2)}) collective-permute-start(bf16[128,2048]{1,0:T(8,128)(2,1)S(1)} %get-tuple-element.98), channel_id=1, source_target_pairs={{0,1},{1,2},{2,3},{4,5},{5,6},{6,7},{8,9},{9,10},{10,11},{12,13},{... | collective-permute-start | bytes 1572872 | tf_op jit(solution)/shard_map/ppermute | solution.py:51
  47.7 15.9 %collective-permute-start.5 = (bf16[128,2048]{1,0:T(8,128)(2,1)S(1)}, bf16[128,2048]{1,0:T(8,128)(2,1)S(1)}, u32[]{:S(2)}, u32[]{:S(2)}) collective-permute-start(bf16[128,2048]{1,0:T(8,128)(2,1)S(1)} %collective-permute-done.4), channel_id=1, source_target_pairs={{2,3},{6,7},{10,11},{14,15},{18,19},{22,23},{26,27},{30,31}} | collective-permute-start | bytes 1572872 | tf_op jit(solution)/shard_map/ppermute | solution.py:51
  68.2 738.9 %reduce-scatter.6.cloned.1.call-start = ((), (), s32[]{:S(2)}) async-start(), calls=%async_computation.7 | async-start | bytes 7962624 | tf_op jit(solution)/shard_map/reduce_scatter | solution.py:192
  148.4 20.0 %collective-permute-start.12 = (bf16[128,2048]{1,0:T(8,128)(2,1)S(1)}, bf16[128,2048]{1,0:T(8,128)(2,1)S(1)}, u32[]{:S(2)}, u32[]{:S(2)}) collective-permute-start(bf16[128,2048]{1,0:T(8,128)(2,1)S(1)} %get-tuple-element.149), channel_id=1, source_target_pairs={{0,1},{4,5},{8,9},{12,13},{16,17},{20,21},{24,25},{28,29}} | collective-permute-start | bytes 1572872 | tf_op jit(solution)/shard_map/ppermute | solution.py:65
  149.8 18.6 %collective-permute-start.15 = (bf16[128,2048]{1,0:T(8,128)(2,1)S(1)}, bf16[128,2048]{1,0:T(8,128)(2,1)S(1)}, u32[]{:S(2)}, u32[]{:S(2)}) collective-permute-start(bf16[128,2048]{1,0:T(8,128)(2,1)S(1)} %get-tuple-element.150), channel_id=1, source_target_pairs={{3,2},{7,6},{11,10},{15,14},{19,18},{23,22},{27,26},{31,30}} | collective-permute-start | bytes 1572872 | tf_op jit(solution)/shard_map/ppermute | solution.py:66
  157.4 22.2 %collective-permute-start.31 = (bf16[128,2048]{1,0:T(8,128)(2,1)S(1)}, bf16[128,2048]{1,0:T(8,128)(2,1)S(1)}, u32[]{:S(2)}, u32[]{:S(2)}) collective-permute-start(bf16[128,2048]{1,0:T(8,128)(2,1)S(1)} %get-tuple-element.153), channel_id=1, source_target_pairs={{0,1},{1,2},{4,5},{5,6},{8,9},{9,10},{12,13},{13,14},{16,17},{17,1... | collective-permute-start | bytes 1572872 | tf_op jit(solution)/shard_map/ppermute | solution.py:65
  161.9 17.8 %collective-permute-start.34 = (bf16[128,2048]{1,0:T(8,128)(2,1)S(1)}, bf16[128,2048]{1,0:T(8,128)(2,1)S(1)}, u32[]{:S(2)}, u32[]{:S(2)}) collective-permute-start(bf16[128,2048]{1,0:T(8,128)(2,1)S(1)} %get-tuple-element.154), channel_id=1, source_target_pairs={{2,1},{3,2},{6,5},{7,6},{10,9},{11,10},{14,13},{15,14},{18,17},{19... | collective-permute-start | bytes 1572872 | tf_op jit(solution)/shard_map/ppermute | solution.py:66
  168.7 22.2 %collective-permute-start.13 = (bf16[128,2048]{1,0:T(8,128)(2,1)S(1)}, bf16[128,2048]{1,0:T(8,128)(2,1)S(1)}, u32[]{:S(2)}, u32[]{:S(2)}) collective-permute-start(bf16[128,2048]{1,0:T(8,128)(2,1)S(1)} %get-tuple-element.147), channel_id=1, source_target_pairs={{0,1},{1,2},{4,5},{5,6},{8,9},{9,10},{12,13},{13,14},{16,17},{17,1... | collective-permute-start | bytes 1572872 | tf_op jit(solution)/shard_map/ppermute | solution.py:65
  173.1 17.8 %collective-permute-start.16 = (bf16[128,2048]{1,0:T(8,128)(2,1)S(1)}, bf16[128,2048]{1,0:T(8,128)(2,1)S(1)}, u32[]{:S(2)}, u32[]{:S(2)}) collective-permute-start(bf16[128,2048]{1,0:T(8,128)(2,1)S(1)} %get-tuple-element.148), channel_id=1, source_target_pairs={{2,1},{3,2},{6,5},{7,6},{10,9},{11,10},{14,13},{15,14},{18,17},{19... | collective-permute-start | bytes 1572872 | tf_op jit(solution)/shard_map/ppermute | solution.py:66
  174.0 23.0 %collective-permute-start.49 = (bf16[128,2048]{1,0:T(8,128)(2,1)S(1)}, bf16[128,2048]{1,0:T(8,128)(2,1)S(1)}, u32[]{:S(2)}, u32[]{:S(2)}) collective-permute-start(bf16[128,2048]{1,0:T(8,128)(2,1)S(1)} %get-tuple-element.167), channel_id=1, source_target_pairs={{1,0},{2,1},{3,2},{5,4},{6,5},{7,6},{9,8},{10,9},{11,10},{13,12},{... | collective-permute-start | bytes 1572872 | tf_op jit(solution)/shard_map/ppermute | solution.py:52
  180.0 25.1 %collective-permute-start.32 = (bf16[128,2048]{1,0:T(8,128)(2,1)S(1)}, bf16[128,2048]{1,0:T(8,128)(2,1)S(1)}, u32[]{:S(2)}, u32[]{:S(2)}) collective-permute-start(bf16[128,2048]{1,0:T(8,128)(2,1)S(1)} %get-tuple-element.151), channel_id=1, source_target_pairs={{0,1},{1,2},{2,3},{4,5},{5,6},{6,7},{8,9},{9,10},{10,11},{12,13},{... | collective-permute-start | bytes 1572872 | tf_op jit(solution)/shard_map/ppermute | solution.py:65
  184.5 22.0 %collective-permute-start.35 = (bf16[128,2048]{1,0:T(8,128)(2,1)S(1)}, bf16[128,2048]{1,0:T(8,128)(2,1)S(1)}, u32[]{:S(2)}, u32[]{:S(2)}) collective-permute-start(bf16[128,2048]{1,0:T(8,128)(2,1)S(1)} %get-tuple-element.152), channel_id=1, source_target_pairs={{1,0},{2,1},{3,2},{5,4},{6,5},{7,6},{9,8},{10,9},{11,10},{13,12},{... | collective-permute-start | bytes 1572872 | tf_op jit(solution)/shard_map/ppermute | solution.py:66
  191.2 22.1 %collective-permute-start.14 = (bf16[128,2048]{1,0:T(8,128)(2,1)S(1)}, bf16[128,2048]{1,0:T(8,128)(2,1)S(1)}, u32[]{:S(2)}, u32[]{:S(2)}) collective-permute-start(bf16[128,2048]{1,0:T(8,128)(2,1)S(1)} %get-tuple-element.145), channel_id=1, source_target_pairs={{0,1},{1,2},{2,3},{4,5},{5,6},{6,7},{8,9},{9,10},{10,11},{12,13},{... | collective-permute-start | bytes 1572872 | tf_op jit(solution)/shard_map/ppermute | solution.py:65
  195.7 17.7 %collective-permute-start.17 = (bf16[128,2048]{1,0:T(8,128)(2,1)S(1)}, bf16[128,2048]{1,0:T(8,128)(2,1)S(1)}, u32[]{:S(2)}, u32[]{:S(2)}) collective-permute-start(bf16[128,2048]{1,0:T(8,128)(2,1)S(1)} %get-tuple-element.146), channel_id=1, source_target_pairs={{1,0},{2,1},{3,2},{5,4},{6,5},{7,6},{9,8},{10,9},{11,10},{13,12},{... | collective-permute-start | bytes 1572872 | tf_op jit(solution)/shard_map/ppermute | solution.py:66
  197.0 22.1 %collective-permute-start.48 = (bf16[128,2048]{1,0:T(8,128)(2,1)S(1)}, bf16[128,2048]{1,0:T(8,128)(2,1)S(1)}, u32[]{:S(2)}, u32[]{:S(2)}) collective-permute-start(bf16[128,2048]{1,0:T(8,128)(2,1)S(1)} %get-tuple-element.167), channel_id=1, source_target_pairs={{0,1},{1,2},{2,3},{4,5},{5,6},{6,7},{8,9},{9,10},{10,11},{12,13},{... | collective-permute-start | bytes 1572872 | tf_op jit(solution)/shard_map/ppermute | solution.py:51
  216.7 21.4 %collective-permute-start.19 = (bf16[128,2048]{1,0:T(8,128)(2,1)S(1)}, bf16[128,2048]{1,0:T(8,128)(2,1)S(1)}, u32[]{:S(2)}, u32[]{:S(2)}) collective-permute-start(bf16[128,2048]{1,0:T(8,128)(2,1)S(1)} %get-tuple-element.72), channel_id=1, source_target_pairs={{1,0},{2,1},{3,2},{5,4},{6,5},{7,6},{9,8},{10,9},{11,10},{13,12},{... | collective-permute-start | bytes 1572872 | tf_op jit(solution)/shard_map/ppermute | solution.py:52
  219.1 20.4 %collective-permute-start.52 = (bf16[128,2048]{1,0:T(8,128)(2,1)S(1)}, bf16[128,2048]{1,0:T(8,128)(2,1)S(1)}, u32[]{:S(2)}, u32[]{:S(2)}) collective-permute-start(bf16[128,2048]{1,0:T(8,128)(2,1)S(1)} %collective-permute-done.48), channel_id=1, source_target_pairs={{1,2},{2,3},{5,6},{6,7},{9,10},{10,11},{13,14},{14,15},{17,18},{18... | collective-permute-start | bytes 1572872 | tf_op jit(solution)/shard_map/ppermute | solution.py:51
  219.8 28.9 %collective-permute-start.51 = (bf16[128,2048]{1,0:T(8,128)(2,1)S(1)}, bf16[128,2048]{1,0:T(8,128)(2,1)S(1)}, u32[]{:S(2)}, u32[]{:S(2)}) collective-permute-start(bf16[128,2048]{1,0:T(8,128)(2,1)S(1)} %collective-permute-done.50), channel_id=1, source_target_pairs={{1,0},{5,4},{9,8},{13,12},{17,16},{21,20},{25,24},{29,28}} | collective-permute-start | bytes 1572872 | tf_op jit(solution)/shard_map/ppermute | solution.py:52
  221.1 28.5 %collective-permute-start.18 = (bf16[128,2048]{1,0:T(8,128)(2,1)S(1)}, bf16[128,2048]{1,0:T(8,128)(2,1)S(1)}, u32[]{:S(2)}, u32[]{:S(2)}) collective-permute-start(bf16[128,2048]{1,0:T(8,128)(2,1)S(1)} %get-tuple-element.72), channel_id=1, source_target_pairs={{0,1},{1,2},{2,3},{4,5},{5,6},{6,7},{8,9},{9,10},{10,11},{12,13},{... | collective-permute-start | bytes 1572872 | tf_op jit(solution)/shard_map/ppermute | solution.py:51
  238.1 17.4 %collective-permute-start.20 = (bf16[128,2048]{1,0:T(8,128)(2,1)S(1)}, bf16[128,2048]{1,0:T(8,128)(2,1)S(1)}, u32[]{:S(2)}, u32[]{:S(2)}) collective-permute-start(bf16[128,2048]{1,0:T(8,128)(2,1)S(1)} %collective-permute-done.19), channel_id=1, source_target_pairs={{1,0},{2,1},{5,4},{6,5},{9,8},{10,9},{13,12},{14,13},{17,16},{18,1... | collective-permute-start | bytes 1572872 | tf_op jit(solution)/shard_map/ppermute | solution.py:52
  239.5 18.3 %collective-permute-start.53 = (bf16[128,2048]{1,0:T(8,128)(2,1)S(1)}, bf16[128,2048]{1,0:T(8,128)(2,1)S(1)}, u32[]{:S(2)}, u32[]{:S(2)}) collective-permute-start(bf16[128,2048]{1,0:T(8,128)(2,1)S(1)} %collective-permute-done.52), channel_id=1, source_target_pairs={{2,3},{6,7},{10,11},{14,15},{18,19},{22,23},{26,27},{30,31}} | collective-permute-start | bytes 1572872 | tf_op jit(solution)/shard_map/ppermute | solution.py:51
  290.9 17.8 %collective-permute-start.24 = (bf16[128,2048]{1,0:T(8,128)(2,1)S(1)}, bf16[128,2048]{1,0:T(8,128)(2,1)S(1)}, u32[]{:S(2)}, u32[]{:S(2)}) collective-permute-start(bf16[128,2048]{1,0:T(8,128)(2,1)S(1)} %get-tuple-element.137), channel_id=1, source_target_pairs={{0,1},{4,5},{8,9},{12,13},{16,17},{20,21},{24,25},{28,29}} | collective-permute-start | bytes 1572872 | tf_op jit(solution)/shard_map/ppermute | solution.py:65
  292.3 16.4 %collective-permute-start.27 = (bf16[128,2048]{1,0:T(8,128)(2,1)S(1)}, bf16[128,2048]{1,0:T(8,128)(2,1)S(1)}, u32[]{:S(2)}, u32[]{:S(2)}) collective-permute-start(bf16[128,2048]{1,0:T(8,128)(2,1)S(1)} %get-tuple-element.138), channel_id=1, source_target_pairs={{3,2},{7,6},{11,10},{15,14},{19,18},{23,22},{27,26},{31,30}} | collective-permute-start | bytes 1572872 | tf_op jit(solution)/shard_map/ppermute | solution.py:66
  300.3 26.6 %collective-permute-start.55 = (bf16[128,2048]{1,0:T(8,128)(2,1)S(1)}, bf16[128,2048]{1,0:T(8,128)(2,1)S(1)}, u32[]{:S(2)}, u32[]{:S(2)}) collective-permute-start(bf16[128,2048]{1,0:T(8,128)(2,1)S(1)} %get-tuple-element.129), channel_id=1, source_target_pairs={{0,1},{1,2},{4,5},{5,6},{8,9},{9,10},{12,13},{13,14},{16,17},{17,1... | collective-permute-start | bytes 1572872 | tf_op jit(solution)/shard_map/ppermute | solution.py:65
  304.7 22.2 %collective-permute-start.58 = (bf16[128,2048]{1,0:T(8,128)(2,1)S(1)}, bf16[128,2048]{1,0:T(8,128)(2,1)S(1)}, u32[]{:S(2)}, u32[]{:S(2)}) collective-permute-start(bf16[128,2048]{1,0:T(8,128)(2,1)S(1)} %get-tuple-element.130), channel_id=1, source_target_pairs={{2,1},{3,2},{6,5},{7,6},{10,9},{11,10},{14,13},{15,14},{18,17},{19... | collective-permute-start | bytes 1572872 | tf_op jit(solution)/shard_map/ppermute | solution.py:66
  309.0 31.6 %collective-permute-start.25 = (bf16[128,2048]{1,0:T(8,128)(2,1)S(1)}, bf16[128,2048]{1,0:T(8,128)(2,1)S(1)}, u32[]{:S(2)}, u32[]{:S(2)}) collective-permute-start(bf16[128,2048]{1,0:T(8,128)(2,1)S(1)} %get-tuple-element.135), channel_id=1, source_target_pairs={{0,1},{1,2},{4,5},{5,6},{8,9},{9,10},{12,13},{13,14},{16,17},{17,1... | collective-permute-start | bytes 1572872 | tf_op jit(solution)/shard_map/ppermute | solution.py:65
  327.3 25.5 %collective-permute-start.56 = (bf16[128,2048]{1,0:T(8,128)(2,1)S(1)}, bf16[128,2048]{1,0:T(8,128)(2,1)S(1)}, u32[]{:S(2)}, u32[]{:S(2)}) collective-permute-start(bf16[128,2048]{1,0:T(8,128)(2,1)S(1)} %get-tuple-element.127), channel_id=1, source_target_pairs={{0,1},{1,2},{2,3},{4,5},{5,6},{6,7},{8,9},{9,10},{10,11},{12,13},{... | collective-permute-start | bytes 1572872 | tf_op jit(solution)/shard_map/ppermute | solution.py:65
  341.1 16.8 %collective-permute-start.26 = (bf16[128,2048]{1,0:T(8,128)(2,1)S(1)}, bf16[128,2048]{1,0:T(8,128)(2,1)S(1)}, u32[]{:S(2)}, u32[]{:S(2)}) collective-permute-start(bf16[128,2048]{1,0:T(8,128)(2,1)S(1)} %get-tuple-element.133), channel_id=1, source_target_pairs={{0,1},{1,2},{2,3},{4,5},{5,6},{6,7},{8,9},{9,10},{10,11},{12,13},{... | collective-permute-start | bytes 1572872 | tf_op jit(solution)/shard_map/ppermute | solution.py:65
  351.2 19.5 %collective-permute-start.29 = (bf16[128,2048]{1,0:T(8,128)(2,1)S(1)}, bf16[128,2048]{1,0:T(8,128)(2,1)S(1)}, u32[]{:S(2)}, u32[]{:S(2)}) collective-permute-start(bf16[128,2048]{1,0:T(8,128)(2,1)S(1)} %get-tuple-element.134), channel_id=1, source_target_pairs={{1,0},{2,1},{3,2},{5,4},{6,5},{7,6},{9,8},{10,9},{11,10},{13,12},{... | collective-permute-start | bytes 1572872 | tf_op jit(solution)/shard_map/ppermute | solution.py:66
  374.9 16.7 %collective-permute-start.67 = (bf16[128,2048]{1,0:T(8,128)(2,1)S(1)}, bf16[128,2048]{1,0:T(8,128)(2,1)S(1)}, u32[]{:S(2)}, u32[]{:S(2)}) collective-permute-start(bf16[128,2048]{1,0:T(8,128)(2,1)S(1)} %get-tuple-element.164), channel_id=1, source_target_pairs={{1,0},{2,1},{3,2},{5,4},{6,5},{7,6},{9,8},{10,9},{11,10},{13,12},{... | collective-permute-start | bytes 1572872 | tf_op jit(solution)/shard_map/ppermute | solution.py:52
  376.2 26.6 %collective-permute-start.61 = (bf16[128,2048]{1,0:T(8,128)(2,1)S(1)}, bf16[128,2048]{1,0:T(8,128)(2,1)S(1)}, u32[]{:S(2)}, u32[]{:S(2)}) collective-permute-start(bf16[128,2048]{1,0:T(8,128)(2,1)S(1)} %get-tuple-element.89), channel_id=1, source_target_pairs={{1,0},{2,1},{3,2},{5,4},{6,5},{7,6},{9,8},{10,9},{11,10},{13,12},{... | collective-permute-start | bytes 1572872 | tf_op jit(solution)/shard_map/ppermute | solution.py:52
  377.5 27.3 %collective-permute-start.66 = (bf16[128,2048]{1,0:T(8,128)(2,1)S(1)}, bf16[128,2048]{1,0:T(8,128)(2,1)S(1)}, u32[]{:S(2)}, u32[]{:S(2)}) collective-permute-start(bf16[128,2048]{1,0:T(8,128)(2,1)S(1)} %get-tuple-element.164), channel_id=1, source_target_pairs={{0,1},{1,2},{2,3},{4,5},{5,6},{6,7},{8,9},{9,10},{10,11},{12,13},{... | collective-permute-start | bytes 1572872 | tf_op jit(solution)/shard_map/ppermute | solution.py:51
  382.7 31.3 %collective-permute-start.37 = (bf16[128,2048]{1,0:T(8,128)(2,1)S(1)}, bf16[128,2048]{1,0:T(8,128)(2,1)S(1)}, u32[]{:S(2)}, u32[]{:S(2)}) collective-permute-start(bf16[128,2048]{1,0:T(8,128)(2,1)S(1)} %get-tuple-element.174), channel_id=1, source_target_pairs={{1,0},{2,1},{3,2},{5,4},{6,5},{7,6},{9,8},{10,9},{11,10},{13,12},{... | collective-permute-start | bytes 1572872 | tf_op jit(solution)/shard_map/ppermute | solution.py:52
  384.0 31.3 %collective-permute-start.36 = (bf16[128,2048]{1,0:T(8,128)(2,1)S(1)}, bf16[128,2048]{1,0:T(8,128)(2,1)S(1)}, u32[]{:S(2)}, u32[]{:S(2)}) collective-permute-start(bf16[128,2048]{1,0:T(8,128)(2,1)S(1)} %get-tuple-element.174), channel_id=1, source_target_pairs={{0,1},{1,2},{2,3},{4,5},{5,6},{6,7},{8,9},{9,10},{10,11},{12,13},{... | collective-permute-start | bytes 1572872 | tf_op jit(solution)/shard_map/ppermute | solution.py:51
  391.5 33.7 %collective-permute-start.68 = (bf16[128,2048]{1,0:T(8,128)(2,1)S(1)}, bf16[128,2048]{1,0:T(8,128)(2,1)S(1)}, u32[]{:S(2)}, u32[]{:S(2)}) collective-permute-start(bf16[128,2048]{1,0:T(8,128)(2,1)S(1)} %collective-permute-done.67), channel_id=1, source_target_pairs={{1,0},{2,1},{5,4},{6,5},{9,8},{10,9},{13,12},{14,13},{17,16},{18,1... | collective-permute-start | bytes 1572872 | tf_op jit(solution)/shard_map/ppermute | solution.py:52
  402.8 23.8 %collective-permute-start.60 = (bf16[128,2048]{1,0:T(8,128)(2,1)S(1)}, bf16[128,2048]{1,0:T(8,128)(2,1)S(1)}, u32[]{:S(2)}, u32[]{:S(2)}) collective-permute-start(bf16[128,2048]{1,0:T(8,128)(2,1)S(1)} %get-tuple-element.89), channel_id=1, source_target_pairs={{0,1},{1,2},{2,3},{4,5},{5,6},{6,7},{8,9},{9,10},{10,11},{12,13},{... | collective-permute-start | bytes 1572872 | tf_op jit(solution)/shard_map/ppermute | solution.py:51
  404.8 23.1 %collective-permute-start.70 = (bf16[128,2048]{1,0:T(8,128)(2,1)S(1)}, bf16[128,2048]{1,0:T(8,128)(2,1)S(1)}, u32[]{:S(2)}, u32[]{:S(2)}) collective-permute-start(bf16[128,2048]{1,0:T(8,128)(2,1)S(1)} %collective-permute-done.66), channel_id=1, source_target_pairs={{1,2},{2,3},{5,6},{6,7},{9,10},{10,11},{13,14},{14,15},{17,18},{18... | collective-permute-start | bytes 1572872 | tf_op jit(solution)/shard_map/ppermute | solution.py:51
  414.0 22.2 %collective-permute-start.38 = (bf16[128,2048]{1,0:T(8,128)(2,1)S(1)}, bf16[128,2048]{1,0:T(8,128)(2,1)S(1)}, u32[]{:S(2)}, u32[]{:S(2)}) collective-permute-start(bf16[128,2048]{1,0:T(8,128)(2,1)S(1)} %collective-permute-done.37), channel_id=1, source_target_pairs={{1,0},{2,1},{5,4},{6,5},{9,8},{10,9},{13,12},{14,13},{17,16},{18,1... | collective-permute-start | bytes 1572872 | tf_op jit(solution)/shard_map/ppermute | solution.py:52
  415.3 21.6 %collective-permute-start.40 = (bf16[128,2048]{1,0:T(8,128)(2,1)S(1)}, bf16[128,2048]{1,0:T(8,128)(2,1)S(1)}, u32[]{:S(2)}, u32[]{:S(2)}) collective-permute-start(bf16[128,2048]{1,0:T(8,128)(2,1)S(1)} %collective-permute-done.36), channel_id=1, source_target_pairs={{1,2},{2,3},{5,6},{6,7},{9,10},{10,11},{13,14},{14,15},{17,18},{18... | collective-permute-start | bytes 1572872 | tf_op jit(solution)/shard_map/ppermute | solution.py:51
  425.3 16.6 %collective-permute-start.69 = (bf16[128,2048]{1,0:T(8,128)(2,1)S(1)}, bf16[128,2048]{1,0:T(8,128)(2,1)S(1)}, u32[]{:S(2)}, u32[]{:S(2)}) collective-permute-start(bf16[128,2048]{1,0:T(8,128)(2,1)S(1)} %collective-permute-done.68), channel_id=1, source_target_pairs={{1,0},{5,4},{9,8},{13,12},{17,16},{21,20},{25,24},{29,28}} | collective-permute-start | bytes 1572872 | tf_op jit(solution)/shard_map/ppermute | solution.py:52
  426.6 59.2 %collective-permute-start.62 = (bf16[128,2048]{1,0:T(8,128)(2,1)S(1)}, bf16[128,2048]{1,0:T(8,128)(2,1)S(1)}, u32[]{:S(2)}, u32[]{:S(2)}) collective-permute-start(bf16[128,2048]{1,0:T(8,128)(2,1)S(1)} %collective-permute-done.61), channel_id=1, source_target_pairs={{1,0},{2,1},{5,4},{6,5},{9,8},{10,9},{13,12},{14,13},{17,16},{18,1... | collective-permute-start | bytes 1572872 | tf_op jit(solution)/shard_map/ppermute | solution.py:52
  427.9 58.6 %collective-permute-start.64 = (bf16[128,2048]{1,0:T(8,128)(2,1)S(1)}, bf16[128,2048]{1,0:T(8,128)(2,1)S(1)}, u32[]{:S(2)}, u32[]{:S(2)}) collective-permute-start(bf16[128,2048]{1,0:T(8,128)(2,1)S(1)} %collective-permute-done.60), channel_id=1, source_target_pairs={{1,2},{2,3},{5,6},{6,7},{9,10},{10,11},{13,14},{14,15},{17,18},{18... | collective-permute-start | bytes 1572872 | tf_op jit(solution)/shard_map/ppermute | solution.py:51
  436.2 18.7 %collective-permute-start.71 = (bf16[128,2048]{1,0:T(8,128)(2,1)S(1)}, bf16[128,2048]{1,0:T(8,128)(2,1)S(1)}, u32[]{:S(2)}, u32[]{:S(2)}) collective-permute-start(bf16[128,2048]{1,0:T(8,128)(2,1)S(1)} %collective-permute-done.70), channel_id=1, source_target_pairs={{2,3},{6,7},{10,11},{14,15},{18,19},{22,23},{26,27},{30,31}} | collective-permute-start | bytes 1572872 | tf_op jit(solution)/shard_map/ppermute | solution.py:51
  436.9 16.2 %collective-permute-start.39 = (bf16[128,2048]{1,0:T(8,128)(2,1)S(1)}, bf16[128,2048]{1,0:T(8,128)(2,1)S(1)}, u32[]{:S(2)}, u32[]{:S(2)}) collective-permute-start(bf16[128,2048]{1,0:T(8,128)(2,1)S(1)} %collective-permute-done.38), channel_id=1, source_target_pairs={{1,0},{5,4},{9,8},{13,12},{17,16},{21,20},{25,24},{29,28}} | collective-permute-start | bytes 1572872 | tf_op jit(solution)/shard_map/ppermute | solution.py:52
  484.4 15.4 %collective-permute-start.72 = (bf16[128,2048]{1,0:T(8,128)(2,1)S(1)}, bf16[128,2048]{1,0:T(8,128)(2,1)S(1)}, u32[]{:S(2)}, u32[]{:S(2)}) collective-permute-start(bf16[128,2048]{1,0:T(8,128)(2,1)S(1)} %get-tuple-element.125), channel_id=1, source_target_pairs={{0,1},{4,5},{8,9},{12,13},{16,17},{20,21},{24,25},{28,29}} | collective-permute-start | bytes 1572872 | tf_op jit(solution)/shard_map/ppermute | solution.py:65
  486.5 19.4 %collective-permute-start.63 = (bf16[128,2048]{1,0:T(8,128)(2,1)S(1)}, bf16[128,2048]{1,0:T(8,128)(2,1)S(1)}, u32[]{:S(2)}, u32[]{:S(2)}) collective-permute-start(bf16[128,2048]{1,0:T(8,128)(2,1)S(1)} %collective-permute-done.62), channel_id=1, source_target_pairs={{1,0},{5,4},{9,8},{13,12},{17,16},{21,20},{25,24},{29,28}} | collective-permute-start | bytes 1572872 | tf_op jit(solution)/shard_map/ppermute | solution.py:52
  488.6 39.8 %collective-permute-start.65 = (bf16[128,2048]{1,0:T(8,128)(2,1)S(1)}, bf16[128,2048]{1,0:T(8,128)(2,1)S(1)}, u32[]{:S(2)}, u32[]{:S(2)}) collective-permute-start(bf16[128,2048]{1,0:T(8,128)(2,1)S(1)} %collective-permute-done.64), channel_id=1, source_target_pairs={{2,3},{6,7},{10,11},{14,15},{18,19},{22,23},{26,27},{30,31}} | collective-permute-start | bytes 1572872 | tf_op jit(solution)/shard_map/ppermute | solution.py:51
  490.0 21.1 %collective-permute-start.43 = (bf16[128,2048]{1,0:T(8,128)(2,1)S(1)}, bf16[128,2048]{1,0:T(8,128)(2,1)S(1)}, u32[]{:S(2)}, u32[]{:S(2)}) collective-permute-start(bf16[128,2048]{1,0:T(8,128)(2,1)S(1)} %get-tuple-element.141), channel_id=1, source_target_pairs={{0,1},{1,2},{4,5},{5,6},{8,9},{9,10},{12,13},{13,14},{16,17},{17,1... | collective-permute-start | bytes 1572872 | tf_op jit(solution)/shard_map/ppermute | solution.py:65
  500.8 20.5 %collective-permute-start.73 = (bf16[128,2048]{1,0:T(8,128)(2,1)S(1)}, bf16[128,2048]{1,0:T(8,128)(2,1)S(1)}, u32[]{:S(2)}, u32[]{:S(2)}) collective-permute-start(bf16[128,2048]{1,0:T(8,128)(2,1)S(1)} %get-tuple-element.123), channel_id=1, source_target_pairs={{0,1},{1,2},{4,5},{5,6},{8,9},{9,10},{12,13},{13,14},{16,17},{17,1... | collective-permute-start | bytes 1572872 | tf_op jit(solution)/shard_map/ppermute | solution.py:65
  505.9 15.5 %collective-permute-start.76 = (bf16[128,2048]{1,0:T(8,128)(2,1)S(1)}, bf16[128,2048]{1,0:T(8,128)(2,1)S(1)}, u32[]{:S(2)}, u32[]{:S(2)}) collective-permute-start(bf16[128,2048]{1,0:T(8,128)(2,1)S(1)} %get-tuple-element.124), channel_id=1, source_target_pairs={{2,1},{3,2},{6,5},{7,6},{10,9},{11,10},{14,13},{15,14},{18,17},{19... | collective-permute-start | bytes 1572872 | tf_op jit(solution)/shard_map/ppermute | solution.py:66
  511.4 17.1 %collective-permute-start.44 = (bf16[128,2048]{1,0:T(8,128)(2,1)S(1)}, bf16[128,2048]{1,0:T(8,128)(2,1)S(1)}, u32[]{:S(2)}, u32[]{:S(2)}) collective-permute-start(bf16[128,2048]{1,0:T(8,128)(2,1)S(1)} %get-tuple-element.139), channel_id=1, source_target_pairs={{0,1},{1,2},{2,3},{4,5},{5,6},{6,7},{8,9},{9,10},{10,11},{12,13},{... | collective-permute-start | bytes 1572872 | tf_op jit(solution)/shard_map/ppermute | solution.py:65
  545.4 15.6 %collective-permute-start.79 = (bf16[128,2048]{1,0:T(8,128)(2,1)S(1)}, bf16[128,2048]{1,0:T(8,128)(2,1)S(1)}, u32[]{:S(2)}, u32[]{:S(2)}) collective-permute-start(bf16[128,2048]{1,0:T(8,128)(2,1)S(1)} %get-tuple-element.86), channel_id=1, source_target_pairs={{1,0},{2,1},{3,2},{5,4},{6,5},{7,6},{9,8},{10,9},{11,10},{13,12},{... | collective-permute-start | bytes 1572872 | tf_op jit(solution)/shard_map/ppermute | solution.py:52
  546.8 15.5 %collective-permute-start.78 = (bf16[128,2048]{1,0:T(8,128)(2,1)S(1)}, bf16[128,2048]{1,0:T(8,128)(2,1)S(1)}, u32[]{:S(2)}, u32[]{:S(2)}) collective-permute-start(bf16[128,2048]{1,0:T(8,128)(2,1)S(1)} %get-tuple-element.86), channel_id=1, source_target_pairs={{0,1},{1,2},{2,3},{4,5},{5,6},{6,7},{8,9},{9,10},{10,11},{12,13},{... | collective-permute-start | bytes 1572872 | tf_op jit(solution)/shard_map/ppermute | solution.py:51
  609.4 202.0 %reduce-scatter.4.cloned.1.call-start = ((), (), s32[]{:S(2)}) async-start(), calls=%async_computation.6 | async-start | bytes 8699904 | tf_op jit(solution)/shard_map/reduce_scatter | solution.py:204
  641.5 194.2 %reduce-scatter.8.cloned.1.call-start = ((), (), s32[]{:S(2)}) async-start(), calls=%async_computation.8 | async-start | bytes 11943936 | tf_op jit(solution)/shard_map/reduce_scatter | solution.py:180
  707.2 16.0 %collective-permute-start.90 = (bf16[128,2048]{1,0:T(8,128)(2,1)S(1)}, bf16[128,2048]{1,0:T(8,128)(2,1)S(1)}, u32[]{:S(2)}, u32[]{:S(2)}) collective-permute-start(bf16[128,2048]{1,0:T(8,128)(2,1)S(1)} %get-tuple-element.119), channel_id=1, source_target_pairs={{0,1},{4,5},{8,9},{12,13},{16,17},{20,21},{24,25},{28,29}} | collective-permute-start | bytes 1572872 | tf_op jit(solution)/shard_map/ppermute | solution.py:65
  712.3 22.1 %collective-permute-start.85 = (bf16[128,2048]{1,0:T(8,128)(2,1)S(1)}, bf16[128,2048]{1,0:T(8,128)(2,1)S(1)}, u32[]{:S(2)}, u32[]{:S(2)}) collective-permute-start(bf16[128,2048]{1,0:T(8,128)(2,1)S(1)} %get-tuple-element.111), channel_id=1, source_target_pairs={{0,1},{1,2},{4,5},{5,6},{8,9},{9,10},{12,13},{13,14},{16,17},{17,1... | collective-permute-start | bytes 1572872 | tf_op jit(solution)/shard_map/ppermute | solution.py:65
  716.7 17.6 %collective-permute-start.88 = (bf16[128,2048]{1,0:T(8,128)(2,1)S(1)}, bf16[128,2048]{1,0:T(8,128)(2,1)S(1)}, u32[]{:S(2)}, u32[]{:S(2)}) collective-permute-start(bf16[128,2048]{1,0:T(8,128)(2,1)S(1)} %get-tuple-element.112), channel_id=1, source_target_pairs={{2,1},{3,2},{6,5},{7,6},{10,9},{11,10},{14,13},{15,14},{18,17},{19... | collective-permute-start | bytes 1572872 | tf_op jit(solution)/shard_map/ppermute | solution.py:66
  723.6 16.9 %collective-permute-start.91 = (bf16[128,2048]{1,0:T(8,128)(2,1)S(1)}, bf16[128,2048]{1,0:T(8,128)(2,1)S(1)}, u32[]{:S(2)}, u32[]{:S(2)}) collective-permute-start(bf16[128,2048]{1,0:T(8,128)(2,1)S(1)} %get-tuple-element.117), channel_id=1, source_target_pairs={{0,1},{1,2},{4,5},{5,6},{8,9},{9,10},{12,13},{13,14},{16,17},{17,1... | collective-permute-start | bytes 1572872 | tf_op jit(solution)/shard_map/ppermute | solution.py:65
  734.8 16.5 %collective-permute-start.86 = (bf16[128,2048]{1,0:T(8,128)(2,1)S(1)}, bf16[128,2048]{1,0:T(8,128)(2,1)S(1)}, u32[]{:S(2)}, u32[]{:S(2)}) collective-permute-start(bf16[128,2048]{1,0:T(8,128)(2,1)S(1)} %get-tuple-element.109), channel_id=1, source_target_pairs={{0,1},{1,2},{2,3},{4,5},{5,6},{6,7},{8,9},{9,10},{10,11},{12,13},{... | collective-permute-start | bytes 1572872 | tf_op jit(solution)/shard_map/ppermute | solution.py:65
  (133 other events, 1992.5 us)
Sparse Core Ops, SparseCore 0:
  12.0 71.3 all-gather.3
  85.3 34.4 all-gather.5
  121.6 65.7 all-gather.7
  609.5 67.7 reduce-scatter.5
  680.6 68.6 reduce-scatter.3
  752.6 83.0 reduce-scatter.7
where the time goes:
time: 856 us; the launch traced here: 847 us
  waiting for transfers between devices  283 us (33%)
  starting transfers between devices  234 us (27%)
  matrix products  159 us (19%)
  other arithmetic  87.5 us (10%)
  blocking collectives  40.4 us (5%)
  local copies, waits for them, and re-layouts  26.1 us (3%)
  between operations  17.2 us (2%)
    ppermute x24, waiting for transfers between devices, line_gather(): l = lax.ppermute(l, 'mp', [(i, i - 1) for i in range(1, n - step + 1)])  154 us
    ppermute x24, starting transfers between devices, line_scatter(): r = lax.ppermute(send_r, 'mp', [(i, i + 1) for i in range(step)])  113 us
    ppermute x24, waiting for transfers between devices, line_scatter(): r = lax.ppermute(send_r, 'mp', [(i, i + 1) for i in range(step)])  79.5 us
    ppermute x24, starting transfers between devices, line_gather(): r = lax.ppermute(r, 'mp', [(i, i + 1) for i in range(step - 1, n - 1)])  66.8 us
    dot_general x5, matrix products, dot_tn(): lax.dot_general(a, b, (((0,), (0,)), ((), ())), preferred_element_type=F32)  51.7 us
    dot_general x8, matrix products, dot_nt(): lax.dot_general(a, b, (((1,), (1,)), ((), ())), preferred_element_type=F32)  48.2 us
    dot_general x8, matrix products, dot_nn(): lax.dot_general(a, b, (((1,), (0,)), ((), ())), preferred_element_type=F32)  43.3 us
    psum x1, blocking collectives, body(): lax.psum(jnp.stack([sum(first_gain), sum(second_gain)]), ('dp', 'mp'))  40.4 us
  transfers between devices with their start and end apart: 102, of which 44 were waited for; matrix products, arithmetic and copies ran while one was open for 24% of the time, Pallas kernels for 0%

commit v1 on v0

--- a/solution.py
+++ b/solution.py
@@ -210,7 +210,9 @@
         input_gradient.append(
             middle_grad[h] + norm_back(first_grad * first_norm_gain, first_hat[h], first_scale[h])
         )
-    gains = lax.psum(jnp.stack([sum(first_gain), sum(second_gain)]), ("dp", "mp"))
+    shard = jnp.stack([sum(first_gain), sum(second_gain)])
+    parts = lax.all_gather(shard, ("dp", "mp"))
+    gains = jnp.sum(parts, axis=0)
     return (
         jnp.concatenate(outputs, axis=0).astype(BF),
         jnp.concatenate(input_gradient, axis=0),

time: 856 us -> 872 us (1.019)
  blocking collectives: 40.4 us -> 75.2 us
  waiting for transfers between devices: 283 us -> 263 us
    all_gather x0 -> x1, blocking collectives: none -> 75.2 us  [body(): parts = lax.all_gather(shard, ('dp', 'mp'))]
    psum x1 -> x0, blocking collectives: 40.4 us -> none  [body(): lax.psum(jnp.stack([sum(first_gain), sum(second_gain)]), ('dp', 'mp'))]
    reduce_scatter x1, waiting for transfers between devices: 19.9 us -> 0.01 us  [body(): lax.psum_scatter(grads_two, 'dp', scatter_dimension=1, tiled=True)]
    unnamed x27 -> x28, other arithmetic: 24.3 us -> 24.3 us
  transfers between devices with their start and end apart: 102 -> 102, of which waited for: 44 -> 43; matrix products, arithmetic and copies ran while one was open for 24% -> 24% of each run, Pallas kernels for 0% -> 0%
where the time goes in v1:
time: 872 us; the launch traced here: 863 us
  waiting for transfers between devices  263 us (30%)
  starting transfers between devices  234 us (27%)
  matrix products  159 us (18%)
  other arithmetic  88.7 us (10%)
  blocking collectives  75.2 us (9%)
  local copies, waits for them, and re-layouts  26.1 us (3%)
  between operations  17.2 us (2%)
    ppermute x24, waiting for transfers between devices, line_gather(): l = lax.ppermute(l, 'mp', [(i, i - 1) for i in range(1, n - step + 1)])  154 us
    ppermute x24, starting transfers between devices, line_scatter(): r = lax.ppermute(send_r, 'mp', [(i, i + 1) for i in range(step)])  113 us
    ppermute x24, waiting for transfers between devices, line_scatter(): r = lax.ppermute(send_r, 'mp', [(i, i + 1) for i in range(step)])  79.5 us
    all_gather x1, blocking collectives, body(): parts = lax.all_gather(shard, ('dp', 'mp'))  75.2 us
    ppermute x24, starting transfers between devices, line_gather(): r = lax.ppermute(r, 'mp', [(i, i + 1) for i in range(step - 1, n - 1)])  66.8 us
    dot_general x5, matrix products, dot_tn(): lax.dot_general(a, b, (((0,), (0,)), ((), ())), preferred_element_type=F32)  51.7 us
    dot_general x8, matrix products, dot_nt(): lax.dot_general(a, b, (((1,), (1,)), ((), ())), preferred_element_type=F32)  48.2 us
    dot_general x8, matrix products, dot_nn(): lax.dot_general(a, b, (((1,), (0,)), ((), ())), preferred_element_type=F32)  43.3 us
  transfers between devices with their start and end apart: 102, of which 43 were waited for; matrix products, arithmetic and copies ran while one was open for 24% of the time, Pallas kernels for 0%

profile of v1, /device:TPU:0, one launch (start us, length us, event | category | flops | bytes accessed | tf_op | source)
XLA Modules:
  0.0 863.0 jit_solution(12415559917782110727)
XLA Ops:
  15.7 5.6 collective-permute-start
  21.3 10.0 %collective-permute-done.1 = bf16[128,2048]{1,0:T(8,128)(2,1)S(1)} collective-permute-done((bf16[128,2048]{1,0:T(8,128)(2,1)S(1)}, bf16[128,2048]{1,0:T(8,128)(2,1)S(1)}, u32[]{:S(2)}, u32[]{:S(2)}) %collective-permute-start.1) | collective-permute-done | bytes 524320 | tf_op jit(solution)/shard_map/ppermute | solution.py:52
  33.3 13.1 %collective-permute-done.2 = bf16[128,2048]{1,0:T(8,128)(2,1)S(1)} collective-permute-done((bf16[128,2048]{1,0:T(8,128)(2,1)S(1)}, bf16[128,2048]{1,0:T(8,128)(2,1)S(1)}, u32[]{:S(2)}, u32[]{:S(2)}) %collective-permute-start.2) | collective-permute-done | bytes 524320 | tf_op jit(solution)/shard_map/ppermute | solution.py:52
  48.6 12.1 %collective-permute-done.3 = bf16[128,2048]{1,0:T(8,128)(2,1)} collective-permute-done((bf16[128,2048]{1,0:T(8,128)(2,1)S(1)}, bf16[128,2048]{1,0:T(8,128)(2,1)}, u32[]{:S(2)}, u32[]{:S(2)}) %collective-permute-start.3) | collective-permute-done | bytes 524320 | tf_op jit(solution)/shard_map/ppermute | solution.py:52
  68.4 4.6 collective-permute-start.6
  73.0 6.1 collective-permute-done.7
  83.5 8.2 collective-permute-done.8
  95.1 8.5 collective-permute-done.9
  107.4 8.1 fusion.74
  118.5 4.9 multiply_convert_fusion.1
  132.7 6.0 fusion.27
  138.7 4.8 convolution_convert_fusion.8
  150.5 6.6 collective-permute-done.30
  162.6 5.8 collective-permute-done.12
  185.8 5.1 collective-permute-done.13
  197.0 8.1 collective-permute-start.48
  206.4 6.9 collective-permute-done.14
  221.1 17.0 %collective-permute-start.18 = (bf16[128,2048]{1,0:T(8,128)(2,1)S(1)}, bf16[128,2048]{1,0:T(8,128)(2,1)S(1)}, u32[]{:S(2)}, u32[]{:S(2)}) collective-permute-start(bf16[128,2048]{1,0:T(8,128)(2,1)S(1)} %get-tuple-element.84), channel_id=1, source_target_pairs={{0,1},{1,2},{2,3},{4,5},{5,6},{6,7},{8,9},{9,10},{10,11},{12,13},{... | collective-permute-start | bytes 1572872 | tf_op jit(solution)/shard_map/ppermute | solution.py:51
  240.2 8.6 collective-permute-done.51
  250.3 5.2 collective-permute-done.20
  259.9 7.3 collective-permute-done.21
  270.7 7.8 fusion.6
  293.0 7.0 collective-permute-done.54
  309.0 16.9 %collective-permute-start.25 = (bf16[128,2048]{1,0:T(8,128)(2,1)S(1)}, bf16[128,2048]{1,0:T(8,128)(2,1)S(1)}, u32[]{:S(2)}, u32[]{:S(2)}) collective-permute-start(bf16[128,2048]{1,0:T(8,128)(2,1)S(1)} %get-tuple-element.147), channel_id=1, source_target_pairs={{0,1},{1,2},{4,5},{5,6},{8,9},{9,10},{12,13},{13,14},{16,17},{17,1... | collective-permute-start | bytes 1572872 | tf_op jit(solution)/shard_map/ppermute | solution.py:65
  327.3 12.0 %collective-permute-start.56 = (bf16[128,2048]{1,0:T(8,128)(2,1)S(1)}, bf16[128,2048]{1,0:T(8,128)(2,1)S(1)}, u32[]{:S(2)}, u32[]{:S(2)}) collective-permute-start(bf16[128,2048]{1,0:T(8,128)(2,1)S(1)} %get-tuple-element.139), channel_id=1, source_target_pairs={{0,1},{1,2},{2,3},{4,5},{5,6},{6,7},{8,9},{9,10},{10,11},{12,13},{... | collective-permute-start | bytes 1572872 | tf_op jit(solution)/shard_map/ppermute | solution.py:65
  341.1 10.1 %collective-permute-start.26 = (bf16[128,2048]{1,0:T(8,128)(2,1)S(1)}, bf16[128,2048]{1,0:T(8,128)(2,1)S(1)}, u32[]{:S(2)}, u32[]{:S(2)}) collective-permute-start(bf16[128,2048]{1,0:T(8,128)(2,1)S(1)} %get-tuple-element.145), channel_id=1, source_target_pairs={{0,1},{1,2},{2,3},{4,5},{5,6},{6,7},{8,9},{9,10},{10,11},{12,13},{... | collective-permute-start | bytes 1572872 | tf_op jit(solution)/shard_map/ppermute | solution.py:65
  357.8 12.8 %collective-permute-done.29 = bf16[128,2048]{1,0:T(8,128)(2,1)S(1)} collective-permute-done((bf16[128,2048]{1,0:T(8,128)(2,1)S(1)}, bf16[128,2048]{1,0:T(8,128)(2,1)S(1)}, u32[]{:S(2)}, u32[]{:S(2)}) %collective-permute-start.29) | collective-permute-done | bytes 524320 | tf_op jit(solution)/shard_map/ppermute | solution.py:66
  377.5 5.2 collective-permute-start.66
  384.0 4.6 collective-permute-start.36
  392.8 9.9 %collective-permute-done.61 = bf16[128,2048]{1,0:T(8,128)(2,1)S(1)} collective-permute-done((bf16[128,2048]{1,0:T(8,128)(2,1)S(1)}, bf16[128,2048]{1,0:T(8,128)(2,1)S(1)}, u32[]{:S(2)}, u32[]{:S(2)}) %collective-permute-start.61) | collective-permute-done | bytes 524320 | tf_op jit(solution)/shard_map/ppermute | solution.py:52
  405.5 8.5 collective-permute-done.37
  416.0 9.2 %collective-permute-done.68 = bf16[128,2048]{1,0:T(8,128)(2,1)S(1)} collective-permute-done((bf16[128,2048]{1,0:T(8,128)(2,1)S(1)}, bf16[128,2048]{1,0:T(8,128)(2,1)S(1)}, u32[]{:S(2)}, u32[]{:S(2)}) %collective-permute-start.68) | collective-permute-done | bytes 524320 | tf_op jit(solution)/shard_map/ppermute | solution.py:52
  428.6 7.7 collective-permute-done.38
  444.4 8.7 %collective-permute-done.39 = bf16[128,2048]{1,0:T(8,128)(2,1)S(1)} collective-permute-done((bf16[128,2048]{1,0:T(8,128)(2,1)S(1)}, bf16[128,2048]{1,0:T(8,128)(2,1)S(1)}, u32[]{:S(2)}, u32[]{:S(2)}) %collective-permute-start.39) | collective-permute-done | bytes 524320 | tf_op jit(solution)/shard_map/ppermute | solution.py:52
  456.8 7.2 fusion.4
  464.0 5.3 fusion.90
  469.4 5.3 convolution_convert_fusion.7
  477.0 7.2 fusion.34
  494.4 5.4 collective-permute-done.72
  500.8 5.0 collective-permute-start.73
  511.4 4.8 collective-permute-start.44
  521.7 5.2 collective-permute-start.74
  529.2 6.3 collective-permute-done.74
  535.5 6.1 collective-permute-done.77
  546.8 7.6 collective-permute-start.78
  554.4 6.6 collective-permute-done.79
  563.0 9.1 %collective-permute-done.80 = bf16[128,2048]{1,0:T(8,128)(2,1)S(1)} collective-permute-done((bf16[128,2048]{1,0:T(8,128)(2,1)S(1)}, bf16[128,2048]{1,0:T(8,128)(2,1)S(1)}, u32[]{:S(2)}, u32[]{:S(2)}) %collective-permute-start.80) | collective-permute-done | bytes 524320 | tf_op jit(solution)/shard_map/ppermute | solution.py:52
  574.1 9.1 %collective-permute-done.81 = bf16[128,2048]{1,0:T(8,128)(2,1)S(1)} collective-permute-done((bf16[128,2048]{1,0:T(8,128)(2,1)S(1)}, bf16[128,2048]{1,0:T(8,128)(2,1)S(1)}, u32[]{:S(2)}, u32[]{:S(2)}) %collective-permute-start.81) | collective-permute-done | bytes 524320 | tf_op jit(solution)/shard_map/ppermute | solution.py:52
  583.6 5.3 convolution_convert_fusion.4
  588.9 6.6 fusion.159
  596.8 5.3 convolution_convert_fusion.3
  602.1 7.3 pad_maximum_fusion.1
  628.1 13.3 %convolution_convert_fusion.1 = bf16[1888,2048]{1,0:T(8,128)(2,1)} fusion(bf16[1024,2048]{1,0:T(8,128)(2,1)S(1)} %copy-done.50, bf16[1024,864]{0,1:T(8,128)(2,1)S(1)} %bitcast.94, bf16[1024,512]{0,1:T(8,128)(2,1)S(1)} %bitcast.102, bf16[1024,512]{0,1:T(8,128)(2,1)S(1)} %bitcast.104), kind=kOutput, calls=%fused_computation.5 | convolution fusion | flops 7934312448 | bytes 15794176 | tf_op jit(solution)/shard_map/dot_general | solution.py:44
  641.8 6.7 convolution_convert_fusion.2
  648.5 21.0 %convolution_convert_fusion = bf16[1728,2048]{1,0:T(8,128)(2,1)S(1)} fusion(bf16[1024,2048]{1,0:T(8,128)(2,1)} %get-tuple-element.69, bf16[512,864]{0,1:T(8,128)(2,1)S(1)} %copy-done.88, bf16[512,864]{0,1:T(8,128)(2,1)S(1)} %copy-done.86, bf16[512,864]{0,1:T(8,128)(2,1)S(1)} %copy-done.84, bf16[512,864]{0,1:T(8,128)(2,1)S(1)} %copy-done.82), kind=kOutput, calls=%fused_computation.4 | convolution fusion | flops 7265452032 | bytes 14811136 | tf_op jit(solution)/shard_map/dot_general | solution.py:44
  669.5 12.8 %pad_maximum_fusion = bf16[2592,2048]{1,0:T(8,128)(2,1)} fusion(bf16[864,2048]{1,0:T(8,128)(2,1)S(1)} %convolution_convert_fusion.2, bf16[1728,2048]{1,0:T(8,128)(2,1)S(1)} %convolution_convert_fusion), kind=kLoop, calls=%fused_computation | loop fusion | flops 21233664 | bytes 21233664 | tf_op jit(solution)/shard_map/concatenate | solution.py:173
  688.1 10.2 %convolution_convert_fusion.6 = bf16[512,2048]{1,0:T(8,128)(2,1)S(1)} fusion(bf16[2752,2048]{1,0:T(8,128)(2,1)} %all-gather.6.cloned.1.call-done, bf16[1024,2752]{0,1:T(8,128)(2,1)S(1)} %pad_maximum_fusion.2), kind=kOutput, calls=%fused_computation.55 | convolution fusion | flops 5772410880 | bytes 16187392 | tf_op jit(solution)/shard_map/dot_general | solution.py:40
  700.5 6.6 convolution_convert_fusion.5
  717.4 5.8 collective-permute-done.90
  723.6 4.5 collective-permute-start.91
  729.0 5.3 collective-permute-done.85
  740.9 7.9 collective-permute-start.92
  755.5 4.4 collective-permute-done.95
  761.2 75.2 %all-gather.1 = f32[32,2,2048]{2,1,0:T(2,128)} all-gather(f32[1,2,2048]{2,1,0:T(2,128)S(1)} %maximum_bitcast_fusion), channel_id=2, replica_groups=mesh['dp'=8,'mp'=4] {'dp','mp'}, dimensions={0}, use_global_device_ids=true | all-gather | bytes 540672 | tf_op jit(solution)/shard_map/all_gather | solution.py:214
  (488 shorter events, 274.0 us)
Async XLA Ops:
  7.2 100.2 %all-gather.6.cloned.1.call-start = ((), (), s32[]{:S(2)}) async-start(), calls=%async_computation.3 | async-start | bytes 12681216 | tf_op jit(solution)/shard_map/all_gather | solution.py:94
  11.9 126.8 %all-gather.8.cloned.1.call-start = ((), (), s32[]{:S(2)}) async-start(), calls=%async_computation.4 | async-start | bytes 3981312 | tf_op jit(solution)/shard_map/all_gather | solution.py:95
  12.6 258.0 %all-gather.10.cloned.1.call-start = ((), (), s32[]{:S(2)}) async-start(), calls=%async_computation.5 | async-start | bytes 11943936 | tf_op jit(solution)/shard_map/all_gather | solution.py:97
  14.4 16.9 %collective-permute-start.1 = (bf16[128,2048]{1,0:T(8,128)(2,1)S(1)}, bf16[128,2048]{1,0:T(8,128)(2,1)S(1)}, u32[]{:S(2)}, u32[]{:S(2)}) collective-permute-start(bf16[128,2048]{1,0:T(8,128)(2,1)S(1)} %get-tuple-element.110), channel_id=1, source_target_pairs={{1,0},{2,1},{3,2},{5,4},{6,5},{7,6},{9,8},{10,9},{11,10},{13,12},{... | collective-permute-start | bytes 1572872 | tf_op jit(solution)/shard_map/ppermute | solution.py:52
  15.7 16.9 %collective-permute-start = (bf16[128,2048]{1,0:T(8,128)(2,1)S(1)}, bf16[128,2048]{1,0:T(8,128)(2,1)S(1)}, u32[]{:S(2)}, u32[]{:S(2)}) collective-permute-start(bf16[128,2048]{1,0:T(8,128)(2,1)S(1)} %get-tuple-element.110), channel_id=1, source_target_pairs={{0,1},{1,2},{2,3},{4,5},{5,6},{6,7},{8,9},{9,10},{10,11},{12,13},{... | collective-permute-start | bytes 1572872 | tf_op jit(solution)/shard_map/ppermute | solution.py:51
  47.7 15.9 %collective-permute-start.5 = (bf16[128,2048]{1,0:T(8,128)(2,1)S(1)}, bf16[128,2048]{1,0:T(8,128)(2,1)S(1)}, u32[]{:S(2)}, u32[]{:S(2)}) collective-permute-start(bf16[128,2048]{1,0:T(8,128)(2,1)S(1)} %collective-permute-done.4), channel_id=1, source_target_pairs={{2,3},{6,7},{10,11},{14,15},{18,19},{22,23},{26,27},{30,31}} | collective-permute-start | bytes 1572872 | tf_op jit(solution)/shard_map/ppermute | solution.py:51
  68.2 774.9 %reduce-scatter.6.cloned.1.call-start = ((), (), s32[]{:S(2)}) async-start(), calls=%async_computation.7 | async-start | bytes 7962624 | tf_op jit(solution)/shard_map/reduce_scatter | solution.py:192
  148.4 20.0 %collective-permute-start.12 = (bf16[128,2048]{1,0:T(8,128)(2,1)S(1)}, bf16[128,2048]{1,0:T(8,128)(2,1)S(1)}, u32[]{:S(2)}, u32[]{:S(2)}) collective-permute-start(bf16[128,2048]{1,0:T(8,128)(2,1)S(1)} %get-tuple-element.161), channel_id=1, source_target_pairs={{0,1},{4,5},{8,9},{12,13},{16,17},{20,21},{24,25},{28,29}} | collective-permute-start | bytes 1572872 | tf_op jit(solution)/shard_map/ppermute | solution.py:65
  149.8 18.6 %collective-permute-start.15 = (bf16[128,2048]{1,0:T(8,128)(2,1)S(1)}, bf16[128,2048]{1,0:T(8,128)(2,1)S(1)}, u32[]{:S(2)}, u32[]{:S(2)}) collective-permute-start(bf16[128,2048]{1,0:T(8,128)(2,1)S(1)} %get-tuple-element.162), channel_id=1, source_target_pairs={{3,2},{7,6},{11,10},{15,14},{19,18},{23,22},{27,26},{31,30}} | collective-permute-start | bytes 1572872 | tf_op jit(solution)/shard_map/ppermute | solution.py:66
  157.4 22.2 %collective-permute-start.31 = (bf16[128,2048]{1,0:T(8,128)(2,1)S(1)}, bf16[128,2048]{1,0:T(8,128)(2,1)S(1)}, u32[]{:S(2)}, u32[]{:S(2)}) collective-permute-start(bf16[128,2048]{1,0:T(8,128)(2,1)S(1)} %get-tuple-element.165), channel_id=1, source_target_pairs={{0,1},{1,2},{4,5},{5,6},{8,9},{9,10},{12,13},{13,14},{16,17},{17,1... | collective-permute-start | bytes 1572872 | tf_op jit(solution)/shard_map/ppermute | solution.py:65
  161.9 17.8 %collective-permute-start.34 = (bf16[128,2048]{1,0:T(8,128)(2,1)S(1)}, bf16[128,2048]{1,0:T(8,128)(2,1)S(1)}, u32[]{:S(2)}, u32[]{:S(2)}) collective-permute-start(bf16[128,2048]{1,0:T(8,128)(2,1)S(1)} %get-tuple-element.166), channel_id=1, source_target_pairs={{2,1},{3,2},{6,5},{7,6},{10,9},{11,10},{14,13},{15,14},{18,17},{19... | collective-permute-start | bytes 1572872 | tf_op jit(solution)/shard_map/ppermute | solution.py:66
  168.7 22.2 %collective-permute-start.13 = (bf16[128,2048]{1,0:T(8,128)(2,1)S(1)}, bf16[128,2048]{1,0:T(8,128)(2,1)S(1)}, u32[]{:S(2)}, u32[]{:S(2)}) collective-permute-start(bf16[128,2048]{1,0:T(8,128)(2,1)S(1)} %get-tuple-element.159), channel_id=1, source_target_pairs={{0,1},{1,2},{4,5},{5,6},{8,9},{9,10},{12,13},{13,14},{16,17},{17,1... | collective-permute-start | bytes 1572872 | tf_op jit(solution)/shard_map/ppermute | solution.py:65
  173.1 17.8 %collective-permute-start.16 = (bf16[128,2048]{1,0:T(8,128)(2,1)S(1)}, bf16[128,2048]{1,0:T(8,128)(2,1)S(1)}, u32[]{:S(2)}, u32[]{:S(2)}) collective-permute-start(bf16[128,2048]{1,0:T(8,128)(2,1)S(1)} %get-tuple-element.160), channel_id=1, source_target_pairs={{2,1},{3,2},{6,5},{7,6},{10,9},{11,10},{14,13},{15,14},{18,17},{19... | collective-permute-start | bytes 1572872 | tf_op jit(solution)/shard_map/ppermute | solution.py:66
  174.0 23.0 %collective-permute-start.49 = (bf16[128,2048]{1,0:T(8,128)(2,1)S(1)}, bf16[128,2048]{1,0:T(8,128)(2,1)S(1)}, u32[]{:S(2)}, u32[]{:S(2)}) collective-permute-start(bf16[128,2048]{1,0:T(8,128)(2,1)S(1)} %get-tuple-element.179), channel_id=1, source_target_pairs={{1,0},{2,1},{3,2},{5,4},{6,5},{7,6},{9,8},{10,9},{11,10},{13,12},{... | collective-permute-start | bytes 1572872 | tf_op jit(solution)/shard_map/ppermute | solution.py:52
  180.0 25.1 %collective-permute-start.32 = (bf16[128,2048]{1,0:T(8,128)(2,1)S(1)}, bf16[128,2048]{1,0:T(8,128)(2,1)S(1)}, u32[]{:S(2)}, u32[]{:S(2)}) collective-permute-start(bf16[128,2048]{1,0:T(8,128)(2,1)S(1)} %get-tuple-element.163), channel_id=1, source_target_pairs={{0,1},{1,2},{2,3},{4,5},{5,6},{6,7},{8,9},{9,10},{10,11},{12,13},{... | collective-permute-start | bytes 1572872 | tf_op jit(solution)/shard_map/ppermute | solution.py:65
  184.5 22.0 %collective-permute-start.35 = (bf16[128,2048]{1,0:T(8,128)(2,1)S(1)}, bf16[128,2048]{1,0:T(8,128)(2,1)S(1)}, u32[]{:S(2)}, u32[]{:S(2)}) collective-permute-start(bf16[128,2048]{1,0:T(8,128)(2,1)S(1)} %get-tuple-element.164), channel_id=1, source_target_pairs={{1,0},{2,1},{3,2},{5,4},{6,5},{7,6},{9,8},{10,9},{11,10},{13,12},{... | collective-permute-start | bytes 1572872 | tf_op jit(solution)/shard_map/ppermute | solution.py:66
  191.2 22.1 %collective-permute-start.14 = (bf16[128,2048]{1,0:T(8,128)(2,1)S(1)}, bf16[128,2048]{1,0:T(8,128)(2,1)S(1)}, u32[]{:S(2)}, u32[]{:S(2)}) collective-permute-start(bf16[128,2048]{1,0:T(8,128)(2,1)S(1)} %get-tuple-element.157), channel_id=1, source_target_pairs={{0,1},{1,2},{2,3},{4,5},{5,6},{6,7},{8,9},{9,10},{10,11},{12,13},{... | collective-permute-start | bytes 1572872 | tf_op jit(solution)/shard_map/ppermute | solution.py:65
  195.7 17.7 %collective-permute-start.17 = (bf16[128,2048]{1,0:T(8,128)(2,1)S(1)}, bf16[128,2048]{1,0:T(8,128)(2,1)S(1)}, u32[]{:S(2)}, u32[]{:S(2)}) collective-permute-start(bf16[128,2048]{1,0:T(8,128)(2,1)S(1)} %get-tuple-element.158), channel_id=1, source_target_pairs={{1,0},{2,1},{3,2},{5,4},{6,5},{7,6},{9,8},{10,9},{11,10},{13,12},{... | collective-permute-start | bytes 1572872 | tf_op jit(solution)/shard_map/ppermute | solution.py:66
  197.0 22.1 %collective-permute-start.48 = (bf16[128,2048]{1,0:T(8,128)(2,1)S(1)}, bf16[128,2048]{1,0:T(8,128)(2,1)S(1)}, u32[]{:S(2)}, u32[]{:S(2)}) collective-permute-start(bf16[128,2048]{1,0:T(8,128)(2,1)S(1)} %get-tuple-element.179), channel_id=1, source_target_pairs={{0,1},{1,2},{2,3},{4,5},{5,6},{6,7},{8,9},{9,10},{10,11},{12,13},{... | collective-permute-start | bytes 1572872 | tf_op jit(solution)/shard_map/ppermute | solution.py:51
  216.7 21.4 %collective-permute-start.19 = (bf16[128,2048]{1,0:T(8,128)(2,1)S(1)}, bf16[128,2048]{1,0:T(8,128)(2,1)S(1)}, u32[]{:S(2)}, u32[]{:S(2)}) collective-permute-start(bf16[128,2048]{1,0:T(8,128)(2,1)S(1)} %get-tuple-element.84), channel_id=1, source_target_pairs={{1,0},{2,1},{3,2},{5,4},{6,5},{7,6},{9,8},{10,9},{11,10},{13,12},{... | collective-permute-start | bytes 1572872 | tf_op jit(solution)/shard_map/ppermute | solution.py:52
  219.1 20.4 %collective-permute-start.52 = (bf16[128,2048]{1,0:T(8,128)(2,1)S(1)}, bf16[128,2048]{1,0:T(8,128)(2,1)S(1)}, u32[]{:S(2)}, u32[]{:S(2)}) collective-permute-start(bf16[128,2048]{1,0:T(8,128)(2,1)S(1)} %collective-permute-done.48), channel_id=1, source_target_pairs={{1,2},{2,3},{5,6},{6,7},{9,10},{10,11},{13,14},{14,15},{17,18},{18... | collective-permute-start | bytes 1572872 | tf_op jit(solution)/shard_map/ppermute | solution.py:51
  219.8 28.9 %collective-permute-start.51 = (bf16[128,2048]{1,0:T(8,128)(2,1)S(1)}, bf16[128,2048]{1,0:T(8,128)(2,1)S(1)}, u32[]{:S(2)}, u32[]{:S(2)}) collective-permute-start(bf16[128,2048]{1,0:T(8,128)(2,1)S(1)} %collective-permute-done.50), channel_id=1, source_target_pairs={{1,0},{5,4},{9,8},{13,12},{17,16},{21,20},{25,24},{29,28}} | collective-permute-start | bytes 1572872 | tf_op jit(solution)/shard_map/ppermute | solution.py:52
  221.1 28.5 %collective-permute-start.18 = (bf16[128,2048]{1,0:T(8,128)(2,1)S(1)}, bf16[128,2048]{1,0:T(8,128)(2,1)S(1)}, u32[]{:S(2)}, u32[]{:S(2)}) collective-permute-start(bf16[128,2048]{1,0:T(8,128)(2,1)S(1)} %get-tuple-element.84), channel_id=1, source_target_pairs={{0,1},{1,2},{2,3},{4,5},{5,6},{6,7},{8,9},{9,10},{10,11},{12,13},{... | collective-permute-start | bytes 1572872 | tf_op jit(solution)/shard_map/ppermute | solution.py:51
  238.1 17.4 %collective-permute-start.20 = (bf16[128,2048]{1,0:T(8,128)(2,1)S(1)}, bf16[128,2048]{1,0:T(8,128)(2,1)S(1)}, u32[]{:S(2)}, u32[]{:S(2)}) collective-permute-start(bf16[128,2048]{1,0:T(8,128)(2,1)S(1)} %collective-permute-done.19), channel_id=1, source_target_pairs={{1,0},{2,1},{5,4},{6,5},{9,8},{10,9},{13,12},{14,13},{17,16},{18,1... | collective-permute-start | bytes 1572872 | tf_op jit(solution)/shard_map/ppermute | solution.py:52
  239.5 18.3 %collective-permute-start.53 = (bf16[128,2048]{1,0:T(8,128)(2,1)S(1)}, bf16[128,2048]{1,0:T(8,128)(2,1)S(1)}, u32[]{:S(2)}, u32[]{:S(2)}) collective-permute-start(bf16[128,2048]{1,0:T(8,128)(2,1)S(1)} %collective-permute-done.52), channel_id=1, source_target_pairs={{2,3},{6,7},{10,11},{14,15},{18,19},{22,23},{26,27},{30,31}} | collective-permute-start | bytes 1572872 | tf_op jit(solution)/shard_map/ppermute | solution.py:51
  290.9 17.8 %collective-permute-start.24 = (bf16[128,2048]{1,0:T(8,128)(2,1)S(1)}, bf16[128,2048]{1,0:T(8,128)(2,1)S(1)}, u32[]{:S(2)}, u32[]{:S(2)}) collective-permute-start(bf16[128,2048]{1,0:T(8,128)(2,1)S(1)} %get-tuple-element.149), channel_id=1, source_target_pairs={{0,1},{4,5},{8,9},{12,13},{16,17},{20,21},{24,25},{28,29}} | collective-permute-start | bytes 1572872 | tf_op jit(solution)/shard_map/ppermute | solution.py:65
  292.3 16.4 %collective-permute-start.27 = (bf16[128,2048]{1,0:T(8,128)(2,1)S(1)}, bf16[128,2048]{1,0:T(8,128)(2,1)S(1)}, u32[]{:S(2)}, u32[]{:S(2)}) collective-permute-start(bf16[128,2048]{1,0:T(8,128)(2,1)S(1)} %get-tuple-element.150), channel_id=1, source_target_pairs={{3,2},{7,6},{11,10},{15,14},{19,18},{23,22},{27,26},{31,30}} | collective-permute-start | bytes 1572872 | tf_op jit(solution)/shard_map/ppermute | solution.py:66
  300.3 26.6 %collective-permute-start.55 = (bf16[128,2048]{1,0:T(8,128)(2,1)S(1)}, bf16[128,2048]{1,0:T(8,128)(2,1)S(1)}, u32[]{:S(2)}, u32[]{:S(2)}) collective-permute-start(bf16[128,2048]{1,0:T(8,128)(2,1)S(1)} %get-tuple-element.141), channel_id=1, source_target_pairs={{0,1},{1,2},{4,5},{5,6},{8,9},{9,10},{12,13},{13,14},{16,17},{17,1... | collective-permute-start | bytes 1572872 | tf_op jit(solution)/shard_map/ppermute | solution.py:65
  304.7 22.2 %collective-permute-start.58 = (bf16[128,2048]{1,0:T(8,128)(2,1)S(1)}, bf16[128,2048]{1,0:T(8,128)(2,1)S(1)}, u32[]{:S(2)}, u32[]{:S(2)}) collective-permute-start(bf16[128,2048]{1,0:T(8,128)(2,1)S(1)} %get-tuple-element.142), channel_id=1, source_target_pairs={{2,1},{3,2},{6,5},{7,6},{10,9},{11,10},{14,13},{15,14},{18,17},{19... | collective-permute-start | bytes 1572872 | tf_op jit(solution)/shard_map/ppermute | solution.py:66
  309.0 31.6 %collective-permute-start.25 = (bf16[128,2048]{1,0:T(8,128)(2,1)S(1)}, bf16[128,2048]{1,0:T(8,128)(2,1)S(1)}, u32[]{:S(2)}, u32[]{:S(2)}) collective-permute-start(bf16[128,2048]{1,0:T(8,128)(2,1)S(1)} %get-tuple-element.147), channel_id=1, source_target_pairs={{0,1},{1,2},{4,5},{5,6},{8,9},{9,10},{12,13},{13,14},{16,17},{17,1... | collective-permute-start | bytes 1572872 | tf_op jit(solution)/shard_map/ppermute | solution.py:65
  327.3 25.5 %collective-permute-start.56 = (bf16[128,2048]{1,0:T(8,128)(2,1)S(1)}, bf16[128,2048]{1,0:T(8,128)(2,1)S(1)}, u32[]{:S(2)}, u32[]{:S(2)}) collective-permute-start(bf16[128,2048]{1,0:T(8,128)(2,1)S(1)} %get-tuple-element.139), channel_id=1, source_target_pairs={{0,1},{1,2},{2,3},{4,5},{5,6},{6,7},{8,9},{9,10},{10,11},{12,13},{... | collective-permute-start | bytes 1572872 | tf_op jit(solution)/shard_map/ppermute | solution.py:65
  341.1 16.8 %collective-permute-start.26 = (bf16[128,2048]{1,0:T(8,128)(2,1)S(1)}, bf16[128,2048]{1,0:T(8,128)(2,1)S(1)}, u32[]{:S(2)}, u32[]{:S(2)}) collective-permute-start(bf16[128,2048]{1,0:T(8,128)(2,1)S(1)} %get-tuple-element.145), channel_id=1, source_target_pairs={{0,1},{1,2},{2,3},{4,5},{5,6},{6,7},{8,9},{9,10},{10,11},{12,13},{... | collective-permute-start | bytes 1572872 | tf_op jit(solution)/shard_map/ppermute | solution.py:65
  351.2 19.5 %collective-permute-start.29 = (bf16[128,2048]{1,0:T(8,128)(2,1)S(1)}, bf16[128,2048]{1,0:T(8,128)(2,1)S(1)}, u32[]{:S(2)}, u32[]{:S(2)}) collective-permute-start(bf16[128,2048]{1,0:T(8,128)(2,1)S(1)} %get-tuple-element.146), channel_id=1, source_target_pairs={{1,0},{2,1},{3,2},{5,4},{6,5},{7,6},{9,8},{10,9},{11,10},{13,12},{... | collective-permute-start | bytes 1572872 | tf_op jit(solution)/shard_map/ppermute | solution.py:66
  374.9 16.7 %collective-permute-start.67 = (bf16[128,2048]{1,0:T(8,128)(2,1)S(1)}, bf16[128,2048]{1,0:T(8,128)(2,1)S(1)}, u32[]{:S(2)}, u32[]{:S(2)}) collective-permute-start(bf16[128,2048]{1,0:T(8,128)(2,1)S(1)} %get-tuple-element.176), channel_id=1, source_target_pairs={{1,0},{2,1},{3,2},{5,4},{6,5},{7,6},{9,8},{10,9},{11,10},{13,12},{... | collective-permute-start | bytes 1572872 | tf_op jit(solution)/shard_map/ppermute | solution.py:52
  376.2 26.6 %collective-permute-start.61 = (bf16[128,2048]{1,0:T(8,128)(2,1)S(1)}, bf16[128,2048]{1,0:T(8,128)(2,1)S(1)}, u32[]{:S(2)}, u32[]{:S(2)}) collective-permute-start(bf16[128,2048]{1,0:T(8,128)(2,1)S(1)} %get-tuple-element.101), channel_id=1, source_target_pairs={{1,0},{2,1},{3,2},{5,4},{6,5},{7,6},{9,8},{10,9},{11,10},{13,12},{... | collective-permute-start | bytes 1572872 | tf_op jit(solution)/shard_map/ppermute | solution.py:52
  377.5 27.3 %collective-permute-start.66 = (bf16[128,2048]{1,0:T(8,128)(2,1)S(1)}, bf16[128,2048]{1,0:T(8,128)(2,1)S(1)}, u32[]{:S(2)}, u32[]{:S(2)}) collective-permute-start(bf16[128,2048]{1,0:T(8,128)(2,1)S(1)} %get-tuple-element.176), channel_id=1, source_target_pairs={{0,1},{1,2},{2,3},{4,5},{5,6},{6,7},{8,9},{9,10},{10,11},{12,13},{... | collective-permute-start | bytes 1572872 | tf_op jit(solution)/shard_map/ppermute | solution.py:51
  382.7 31.3 %collective-permute-start.37 = (bf16[128,2048]{1,0:T(8,128)(2,1)S(1)}, bf16[128,2048]{1,0:T(8,128)(2,1)S(1)}, u32[]{:S(2)}, u32[]{:S(2)}) collective-permute-start(bf16[128,2048]{1,0:T(8,128)(2,1)S(1)} %get-tuple-element.186), channel_id=1, source_target_pairs={{1,0},{2,1},{3,2},{5,4},{6,5},{7,6},{9,8},{10,9},{11,10},{13,12},{... | collective-permute-start | bytes 1572872 | tf_op jit(solution)/shard_map/ppermute | solution.py:52
  384.0 31.3 %collective-permute-start.36 = (bf16[128,2048]{1,0:T(8,128)(2,1)S(1)}, bf16[128,2048]{1,0:T(8,128)(2,1)S(1)}, u32[]{:S(2)}, u32[]{:S(2)}) collective-permute-start(bf16[128,2048]{1,0:T(8,128)(2,1)S(1)} %get-tuple-element.186), channel_id=1, source_target_pairs={{0,1},{1,2},{2,3},{4,5},{5,6},{6,7},{8,9},{9,10},{10,11},{12,13},{... | collective-permute-start | bytes 1572872 | tf_op jit(solution)/shard_map/ppermute | solution.py:51
  391.5 33.7 %collective-permute-start.68 = (bf16[128,2048]{1,0:T(8,128)(2,1)S(1)}, bf16[128,2048]{1,0:T(8,128)(2,1)S(1)}, u32[]{:S(2)}, u32[]{:S(2)}) collective-permute-start(bf16[128,2048]{1,0:T(8,128)(2,1)S(1)} %collective-permute-done.67), channel_id=1, source_target_pairs={{1,0},{2,1},{5,4},{6,5},{9,8},{10,9},{13,12},{14,13},{17,16},{18,1... | collective-permute-start | bytes 1572872 | tf_op jit(solution)/shard_map/ppermute | solution.py:52
  402.8 23.8 %collective-permute-start.60 = (bf16[128,2048]{1,0:T(8,128)(2,1)S(1)}, bf16[128,2048]{1,0:T(8,128)(2,1)S(1)}, u32[]{:S(2)}, u32[]{:S(2)}) collective-permute-start(bf16[128,2048]{1,0:T(8,128)(2,1)S(1)} %get-tuple-element.101), channel_id=1, source_target_pairs={{0,1},{1,2},{2,3},{4,5},{5,6},{6,7},{8,9},{9,10},{10,11},{12,13},{... | collective-permute-start | bytes 1572872 | tf_op jit(solution)/shard_map/ppermute | solution.py:51
  404.8 23.1 %collective-permute-start.70 = (bf16[128,2048]{1,0:T(8,128)(2,1)S(1)}, bf16[128,2048]{1,0:T(8,128)(2,1)S(1)}, u32[]{:S(2)}, u32[]{:S(2)}) collective-permute-start(bf16[128,2048]{1,0:T(8,128)(2,1)S(1)} %collective-permute-done.66), channel_id=1, source_target_pairs={{1,2},{2,3},{5,6},{6,7},{9,10},{10,11},{13,14},{14,15},{17,18},{18... | collective-permute-start | bytes 1572872 | tf_op jit(solution)/shard_map/ppermute | solution.py:51
  414.0 22.2 %collective-permute-start.38 = (bf16[128,2048]{1,0:T(8,128)(2,1)S(1)}, bf16[128,2048]{1,0:T(8,128)(2,1)S(1)}, u32[]{:S(2)}, u32[]{:S(2)}) collective-permute-start(bf16[128,2048]{1,0:T(8,128)(2,1)S(1)} %collective-permute-done.37), channel_id=1, source_target_pairs={{1,0},{2,1},{5,4},{6,5},{9,8},{10,9},{13,12},{14,13},{17,16},{18,1... | collective-permute-start | bytes 1572872 | tf_op jit(solution)/shard_map/ppermute | solution.py:52
  415.3 21.6 %collective-permute-start.40 = (bf16[128,2048]{1,0:T(8,128)(2,1)S(1)}, bf16[128,2048]{1,0:T(8,128)(2,1)S(1)}, u32[]{:S(2)}, u32[]{:S(2)}) collective-permute-start(bf16[128,2048]{1,0:T(8,128)(2,1)S(1)} %collective-permute-done.36), channel_id=1, source_target_pairs={{1,2},{2,3},{5,6},{6,7},{9,10},{10,11},{13,14},{14,15},{17,18},{18... | collective-permute-start | bytes 1572872 | tf_op jit(solution)/shard_map/ppermute | solution.py:51
  425.3 16.6 %collective-permute-start.69 = (bf16[128,2048]{1,0:T(8,128)(2,1)S(1)}, bf16[128,2048]{1,0:T(8,128)(2,1)S(1)}, u32[]{:S(2)}, u32[]{:S(2)}) collective-permute-start(bf16[128,2048]{1,0:T(8,128)(2,1)S(1)} %collective-permute-done.68), channel_id=1, source_target_pairs={{1,0},{5,4},{9,8},{13,12},{17,16},{21,20},{25,24},{29,28}} | collective-permute-start | bytes 1572872 | tf_op jit(solution)/shard_map/ppermute | solution.py:52
  426.6 59.2 %collective-permute-start.62 = (bf16[128,2048]{1,0:T(8,128)(2,1)S(1)}, bf16[128,2048]{1,0:T(8,128)(2,1)S(1)}, u32[]{:S(2)}, u32[]{:S(2)}) collective-permute-start(bf16[128,2048]{1,0:T(8,128)(2,1)S(1)} %collective-permute-done.61), channel_id=1, source_target_pairs={{1,0},{2,1},{5,4},{6,5},{9,8},{10,9},{13,12},{14,13},{17,16},{18,1... | collective-permute-start | bytes 1572872 | tf_op jit(solution)/shard_map/ppermute | solution.py:52
  427.9 58.6 %collective-permute-start.64 = (bf16[128,2048]{1,0:T(8,128)(2,1)S(1)}, bf16[128,2048]{1,0:T(8,128)(2,1)S(1)}, u32[]{:S(2)}, u32[]{:S(2)}) collective-permute-start(bf16[128,2048]{1,0:T(8,128)(2,1)S(1)} %collective-permute-done.60), channel_id=1, source_target_pairs={{1,2},{2,3},{5,6},{6,7},{9,10},{10,11},{13,14},{14,15},{17,18},{18... | collective-permute-start | bytes 1572872 | tf_op jit(solution)/shard_map/ppermute | solution.py:51
  436.2 18.7 %collective-permute-start.71 = (bf16[128,2048]{1,0:T(8,128)(2,1)S(1)}, bf16[128,2048]{1,0:T(8,128)(2,1)S(1)}, u32[]{:S(2)}, u32[]{:S(2)}) collective-permute-start(bf16[128,2048]{1,0:T(8,128)(2,1)S(1)} %collective-permute-done.70), channel_id=1, source_target_pairs={{2,3},{6,7},{10,11},{14,15},{18,19},{22,23},{26,27},{30,31}} | collective-permute-start | bytes 1572872 | tf_op jit(solution)/shard_map/ppermute | solution.py:51
  436.9 16.2 %collective-permute-start.39 = (bf16[128,2048]{1,0:T(8,128)(2,1)S(1)}, bf16[128,2048]{1,0:T(8,128)(2,1)S(1)}, u32[]{:S(2)}, u32[]{:S(2)}) collective-permute-start(bf16[128,2048]{1,0:T(8,128)(2,1)S(1)} %collective-permute-done.38), channel_id=1, source_target_pairs={{1,0},{5,4},{9,8},{13,12},{17,16},{21,20},{25,24},{29,28}} | collective-permute-start | bytes 1572872 | tf_op jit(solution)/shard_map/ppermute | solution.py:52
  484.4 15.4 %collective-permute-start.72 = (bf16[128,2048]{1,0:T(8,128)(2,1)S(1)}, bf16[128,2048]{1,0:T(8,128)(2,1)S(1)}, u32[]{:S(2)}, u32[]{:S(2)}) collective-permute-start(bf16[128,2048]{1,0:T(8,128)(2,1)S(1)} %get-tuple-element.137), channel_id=1, source_target_pairs={{0,1},{4,5},{8,9},{12,13},{16,17},{20,21},{24,25},{28,29}} | collective-permute-start | bytes 1572872 | tf_op jit(solution)/shard_map/ppermute | solution.py:65
  486.5 19.4 %collective-permute-start.63 = (bf16[128,2048]{1,0:T(8,128)(2,1)S(1)}, bf16[128,2048]{1,0:T(8,128)(2,1)S(1)}, u32[]{:S(2)}, u32[]{:S(2)}) collective-permute-start(bf16[128,2048]{1,0:T(8,128)(2,1)S(1)} %collective-permute-done.62), channel_id=1, source_target_pairs={{1,0},{5,4},{9,8},{13,12},{17,16},{21,20},{25,24},{29,28}} | collective-permute-start | bytes 1572872 | tf_op jit(solution)/shard_map/ppermute | solution.py:52
  488.6 39.8 %collective-permute-start.65 = (bf16[128,2048]{1,0:T(8,128)(2,1)S(1)}, bf16[128,2048]{1,0:T(8,128)(2,1)S(1)}, u32[]{:S(2)}, u32[]{:S(2)}) collective-permute-start(bf16[128,2048]{1,0:T(8,128)(2,1)S(1)} %collective-permute-done.64), channel_id=1, source_target_pairs={{2,3},{6,7},{10,11},{14,15},{18,19},{22,23},{26,27},{30,31}} | collective-permute-start | bytes 1572872 | tf_op jit(solution)/shard_map/ppermute | solution.py:51
  490.0 21.1 %collective-permute-start.43 = (bf16[128,2048]{1,0:T(8,128)(2,1)S(1)}, bf16[128,2048]{1,0:T(8,128)(2,1)S(1)}, u32[]{:S(2)}, u32[]{:S(2)}) collective-permute-start(bf16[128,2048]{1,0:T(8,128)(2,1)S(1)} %get-tuple-element.153), channel_id=1, source_target_pairs={{0,1},{1,2},{4,5},{5,6},{8,9},{9,10},{12,13},{13,14},{16,17},{17,1... | collective-permute-start | bytes 1572872 | tf_op jit(solution)/shard_map/ppermute | solution.py:65
  500.8 20.5 %collective-permute-start.73 = (bf16[128,2048]{1,0:T(8,128)(2,1)S(1)}, bf16[128,2048]{1,0:T(8,128)(2,1)S(1)}, u32[]{:S(2)}, u32[]{:S(2)}) collective-permute-start(bf16[128,2048]{1,0:T(8,128)(2,1)S(1)} %get-tuple-element.135), channel_id=1, source_target_pairs={{0,1},{1,2},{4,5},{5,6},{8,9},{9,10},{12,13},{13,14},{16,17},{17,1... | collective-permute-start | bytes 1572872 | tf_op jit(solution)/shard_map/ppermute | solution.py:65
  505.9 15.5 %collective-permute-start.76 = (bf16[128,2048]{1,0:T(8,128)(2,1)S(1)}, bf16[128,2048]{1,0:T(8,128)(2,1)S(1)}, u32[]{:S(2)}, u32[]{:S(2)}) collective-permute-start(bf16[128,2048]{1,0:T(8,128)(2,1)S(1)} %get-tuple-element.136), channel_id=1, source_target_pairs={{2,1},{3,2},{6,5},{7,6},{10,9},{11,10},{14,13},{15,14},{18,17},{19... | collective-permute-start | bytes 1572872 | tf_op jit(solution)/shard_map/ppermute | solution.py:66
  511.4 17.1 %collective-permute-start.44 = (bf16[128,2048]{1,0:T(8,128)(2,1)S(1)}, bf16[128,2048]{1,0:T(8,128)(2,1)S(1)}, u32[]{:S(2)}, u32[]{:S(2)}) collective-permute-start(bf16[128,2048]{1,0:T(8,128)(2,1)S(1)} %get-tuple-element.151), channel_id=1, source_target_pairs={{0,1},{1,2},{2,3},{4,5},{5,6},{6,7},{8,9},{9,10},{10,11},{12,13},{... | collective-permute-start | bytes 1572872 | tf_op jit(solution)/shard_map/ppermute | solution.py:65
  545.4 15.6 %collective-permute-start.79 = (bf16[128,2048]{1,0:T(8,128)(2,1)S(1)}, bf16[128,2048]{1,0:T(8,128)(2,1)S(1)}, u32[]{:S(2)}, u32[]{:S(2)}) collective-permute-start(bf16[128,2048]{1,0:T(8,128)(2,1)S(1)} %get-tuple-element.98), channel_id=1, source_target_pairs={{1,0},{2,1},{3,2},{5,4},{6,5},{7,6},{9,8},{10,9},{11,10},{13,12},{... | collective-permute-start | bytes 1572872 | tf_op jit(solution)/shard_map/ppermute | solution.py:52
  546.8 15.5 %collective-permute-start.78 = (bf16[128,2048]{1,0:T(8,128)(2,1)S(1)}, bf16[128,2048]{1,0:T(8,128)(2,1)S(1)}, u32[]{:S(2)}, u32[]{:S(2)}) collective-permute-start(bf16[128,2048]{1,0:T(8,128)(2,1)S(1)} %get-tuple-element.98), channel_id=1, source_target_pairs={{0,1},{1,2},{2,3},{4,5},{5,6},{6,7},{8,9},{9,10},{10,11},{12,13},{... | collective-permute-start | bytes 1572872 | tf_op jit(solution)/shard_map/ppermute | solution.py:51
  609.4 238.1 %reduce-scatter.4.cloned.1.call-start = ((), (), s32[]{:S(2)}) async-start(), calls=%async_computation.6 | async-start | bytes 8699904 | tf_op jit(solution)/shard_map/reduce_scatter | solution.py:204
  641.5 210.3 %reduce-scatter.8.cloned.1.call-start = ((), (), s32[]{:S(2)}) async-start(), calls=%async_computation.8 | async-start | bytes 11943936 | tf_op jit(solution)/shard_map/reduce_scatter | solution.py:180
  707.2 16.0 %collective-permute-start.90 = (bf16[128,2048]{1,0:T(8,128)(2,1)S(1)}, bf16[128,2048]{1,0:T(8,128)(2,1)S(1)}, u32[]{:S(2)}, u32[]{:S(2)}) collective-permute-start(bf16[128,2048]{1,0:T(8,128)(2,1)S(1)} %get-tuple-element.131), channel_id=1, source_target_pairs={{0,1},{4,5},{8,9},{12,13},{16,17},{20,21},{24,25},{28,29}} | collective-permute-start | bytes 1572872 | tf_op jit(solution)/shard_map/ppermute | solution.py:65
  712.3 22.1 %collective-permute-start.85 = (bf16[128,2048]{1,0:T(8,128)(2,1)S(1)}, bf16[128,2048]{1,0:T(8,128)(2,1)S(1)}, u32[]{:S(2)}, u32[]{:S(2)}) collective-permute-start(bf16[128,2048]{1,0:T(8,128)(2,1)S(1)} %get-tuple-element.123), channel_id=1, source_target_pairs={{0,1},{1,2},{4,5},{5,6},{8,9},{9,10},{12,13},{13,14},{16,17},{17,1... | collective-permute-start | bytes 1572872 | tf_op jit(solution)/shard_map/ppermute | solution.py:65
  716.7 17.6 %collective-permute-start.88 = (bf16[128,2048]{1,0:T(8,128)(2,1)S(1)}, bf16[128,2048]{1,0:T(8,128)(2,1)S(1)}, u32[]{:S(2)}, u32[]{:S(2)}) collective-permute-start(bf16[128,2048]{1,0:T(8,128)(2,1)S(1)} %get-tuple-element.124), channel_id=1, source_target_pairs={{2,1},{3,2},{6,5},{7,6},{10,9},{11,10},{14,13},{15,14},{18,17},{19... | collective-permute-start | bytes 1572872 | tf_op jit(solution)/shard_map/ppermute | solution.py:66
  723.6 16.9 %collective-permute-start.91 = (bf16[128,2048]{1,0:T(8,128)(2,1)S(1)}, bf16[128,2048]{1,0:T(8,128)(2,1)S(1)}, u32[]{:S(2)}, u32[]{:S(2)}) collective-permute-start(bf16[128,2048]{1,0:T(8,128)(2,1)S(1)} %get-tuple-element.129), channel_id=1, source_target_pairs={{0,1},{1,2},{4,5},{5,6},{8,9},{9,10},{12,13},{13,14},{16,17},{17,1... | collective-permute-start | bytes 1572872 | tf_op jit(solution)/shard_map/ppermute | solution.py:65
  734.8 16.5 %collective-permute-start.86 = (bf16[128,2048]{1,0:T(8,128)(2,1)S(1)}, bf16[128,2048]{1,0:T(8,128)(2,1)S(1)}, u32[]{:S(2)}, u32[]{:S(2)}) collective-permute-start(bf16[128,2048]{1,0:T(8,128)(2,1)S(1)} %get-tuple-element.121), channel_id=1, source_target_pairs={{0,1},{1,2},{2,3},{4,5},{5,6},{6,7},{8,9},{9,10},{10,11},{12,13},{... | collective-permute-start | bytes 1572872 | tf_op jit(solution)/shard_map/ppermute | solution.py:65
  (133 other events, 1992.5 us)
Sparse Core Ops, SparseCore 0:
  12.0 71.3 all-gather.5
  85.3 34.4 all-gather.7
  121.6 65.7 all-gather.9
  609.5 67.7 reduce-scatter.5
  680.6 68.6 reduce-scatter.3
  752.6 84.0 reduce-scatter.7
